TPU v7x, 128 devices: a whole 4x4x4 slice. The times are simulated.
128 devices in a mesh: grp: 4 (over x), seq: 32 (over y, z, core).
Axes of the slice: x: 4, y: 4, z: 4, core: 2. Of those that a mesh axis runs over, the one named last changes fastest.
Arguments:
- tokens: bfloat16 [8192, 8192], P(None, 'seq'), may hold values from -16 to 16
- proj_weight: bfloat16 [8192, 5120], P('seq', 'grp'), may hold values from -0.0625 to 0.0625
- proj_bias: bfloat16 [5120], P('grp'), may hold values from -3 to 3
- out_weight: bfloat16 [4096, 8192], P('grp'), may hold values from -0.125 to 0.125
- doc_ids: int32 [8192], P('seq'), may hold values from 0 to 2, never falling along the last dimension, each value on 1 to 4352 neighbouring positions
Outputs:
- mixed: bfloat16 [8192, 8192], P('seq', 'grp')
Inputs may be any that keep to these rules, and one draw needn't show every extreme that they name: `doc_ids`: numbers never fall along the sequence; every document has 1 to 4352 tokens, one exactly that many; every number up to 2 is used.
All inputs are finite; a program needn't handle non-finite values.
Results may differ from a plain program's by a relative error of at most 0.012.
Values may be sent and summed in bfloat16 or wider, within the bound.
No kernel may reach another device: no remote copies, remote signals or barrier semaphores. Data moves between devices by JAX's collectives and lax.ppermute only.
A program may use at most 256 MiB of HBM per device.

v0:
```python
import jax
import jax.numpy as jnp
from jax import lax
from jax.sharding import PartitionSpec as P

HEAD_DIM = 128
GQA = 8


theta_base = 1000000.0
neg_large = -1e30


def in_one_piece(arrays, axis, dim, along):
    widths = [a.shape[along] for a in arrays]
    both = jnp.concatenate(arrays, axis=along)
    filled = lax.all_gather(both, axis, axis=dim, tiled=True)
    return tuple(jnp.split(filled, [sum(widths[:k]) for k in range(1, len(widths))], axis=along))


def rotate(inputs, positions, head_dim):
    half_dim = head_dim // 2
    inverse_freq = theta_base ** (-(jnp.arange(half_dim, dtype=jnp.float32) * 2.0) / head_dim)
    angles = positions.astype(jnp.float32)[:, None] * inverse_freq[None, :]
    cosine = jnp.concatenate([jnp.cos(angles), jnp.cos(angles)], axis=1)
    sine_table = jnp.concatenate([jnp.sin(angles), jnp.sin(angles)], axis=1)
    low_half = inputs[..., :half_dim]
    high_half = inputs[..., half_dim:]
    turned = jnp.concatenate([-high_half, low_half], axis=-1)
    return inputs * cosine[:, None, :] + turned * sine_table[:, None, :]


def body(tokens, proj_weight, proj_bias, out_weight, doc_ids):
    tok_rows = doc_ids.shape[0]
    kv_local = proj_weight.shape[1] // ((GQA + 2) * HEAD_DIM)
    my_start = lax.axis_index("seq") * tok_rows
    own_rows = lax.all_to_all(tokens, "seq", split_axis=0, concat_axis=1, tiled=True)
    projected = jnp.dot(
        own_rows,
        lax.all_gather(proj_weight, "seq", axis=0, tiled=True),
        preferred_element_type=jnp.float32,
    )
    projected = projected + proj_bias.astype(jnp.float32)[None, :]
    projected = projected.reshape(tok_rows, kv_local, GQA + 2, HEAD_DIM)
    positions = my_start + jnp.arange(tok_rows, dtype=jnp.int32)
    queries = rotate(
        projected[:, :, :GQA, :].reshape(tok_rows, kv_local * GQA, HEAD_DIM), positions, HEAD_DIM
    )
    queries = queries.astype(jnp.bfloat16).reshape(tok_rows, kv_local, GQA, HEAD_DIM)
    key_rows = rotate(projected[:, :, GQA, :], positions, HEAD_DIM).astype(jnp.bfloat16)
    value_rows = projected[:, :, GQA + 1, :].astype(jnp.bfloat16)
    score_scale = HEAD_DIM ** (-0.5)
    initial = (
        jnp.full((kv_local, GQA, tok_rows), neg_large, jnp.float32),
        jnp.zeros((kv_local, GQA, tok_rows), jnp.float32),
        jnp.zeros((kv_local, GQA, tok_rows, HEAD_DIM), jnp.float32),
    )
    key_block, value_block, block_ids = (
        *in_one_piece((key_rows, value_rows), "seq", 0, 1),
        lax.all_gather(doc_ids, "seq", axis=0, tiled=True),
    )
    key_index = jnp.arange(block_ids.shape[0], dtype=jnp.int32)
    allowed = (
        (block_ids[None, :] == doc_ids[:, None])
        & (key_index[None, :] <= positions[:, None])
        & (key_index[None, :] >= 0)
    )

    def compute(state):
        row_max, row_sum, weighted = state
        scores = (
            jnp.einsum("qkgd,pkd->kgqp", queries, key_block, preferred_element_type=jnp.float32)
            * score_scale
        )
        scores = jnp.where(allowed[None, None], scores, neg_large)
        new_max = jnp.maximum(row_max, jnp.max(scores, axis=-1))
        weights = jnp.where(allowed[None, None], jnp.exp(scores - new_max[..., None]), 0.0)
        new_sum = jnp.sum(weights, axis=-1)
        update = jnp.einsum(
            "kgqp,pkd->kgqd",
            weights.astype(jnp.bfloat16),
            value_block,
            preferred_element_type=jnp.float32,
        )
        return (new_max, new_sum, update)

    folded = lax.cond(jnp.any(allowed), compute, lambda state: state, initial)
    row_max, row_sum, weighted = folded
    outputs = (weighted / row_sum[..., None]).astype(jnp.bfloat16)
    attended = jnp.transpose(outputs, (2, 0, 1, 3)).reshape(tok_rows, kv_local * GQA * HEAD_DIM)
    partial_value = jnp.dot(attended, out_weight, preferred_element_type=jnp.float32)
    return lax.psum_scatter(partial_value, "grp", scatter_dimension=1, tiled=True).astype(
        jnp.bfloat16
    )


def solution(mesh):
    return jax.shard_map(
        body,
        mesh=mesh,
        in_specs=(P(None, "seq"), P("seq", "grp"), P("grp"), P("grp", None), P("seq")),
        out_specs=P("seq", "grp"),
        check_vma=False,
    )
```

profile of v0, /device:TPU:24, one launch (start us, length us, event | category | flops | bytes accessed | tf_op | source)
XLA Modules:
  0.0 373.0 jit_solution(14919422232318146023)
XLA Ops:
  6.5 0.7 all-gather.4.cloned.1.call-update
  7.3 8.4 %all-to-all-start = ((bf16[32,256,256]{2,1,0:T(8,128)(2,1)}), bf16[32,256,256]{2,1,0:T(8,128)(2,1)}, u32[]{:S(2)}, u32[]{:S(2)}) async-start(bf16[32,256,256]{2,1,0:T(8,128)(2,1)} %bitcast.80), calls=%async_computation | async-start | bytes 8388608 | tf_op jit(solution)/shard_map/all_to_all | solution.py:37
  15.8 0.3 multiply_cosine_fusion
  16.1 58.3 %all-to-all-done = bf16[32,256,256]{2,1,0:T(8,128)(2,1)} async-done(((bf16[32,256,256]{2,1,0:T(8,128)(2,1)}), bf16[32,256,256]{2,1,0:T(8,128)(2,1)}, u32[]{:S(2)}, u32[]{:S(2)}) %all-to-all-start) | async-done | bytes 4194336 | tf_op jit(solution)/shard_map/all_to_all | solution.py:37
  74.5 6.5 %copy.22 = bf16[256,32,256]{0,2,1:T(8,128)(2,1)} copy(bf16[256,32,256]{2,0,1:T(8,128)(2,1)} %bitcast.13) | data formatting | bytes 8388608 | tf_op jit(solution)/shard_map/all_to_all | solution.py:37
  80.9 50.4 %all-gather.4.cloned.1.call-done = bf16[8192,1280]{1,0:T(8,128)(2,1)} async-done(((bf16[256,1280]{1,0:T(8,128)(2,1)}), bf16[8192,1280]{1,0:T(8,128)(2,1)}) %all-gather.4.cloned.1.call-update) | async-done | bytes 20971536 | tf_op jit(solution)/shard_map/all_gather | solution.py:40
  131.3 12.2 %convolution_add_fusion = f32[256,1280]{1,0:T(8,128)S(1)} fusion(bf16[256,8192]{0,1:T(8,128)(2,1)} %bitcast.74, bf16[8192,1280]{1,0:T(8,128)(2,1)} %all-gather.4.cloned.1.call-done, f32[1280]{0:T(1024)S(1)} %convert_element_type.51), kind=kOutput, calls=%fused_computation.19 | convolution fusion | flops 5369036800 | bytes 26481664 | tf_op jit(solution)/shard_map/dot_general | solution.py:38
  143.6 0.4 copy.23
  144.1 0.7 pad_maximum_fusion
  144.8 22.0 %all-gather = s32[32,1,256]{2,1,0:T(1,128)S(1)} all-gather(s32[1,1,256]{2,1,0:T(1,128)S(1)} %bitcast.85), channel_id=1, replica_groups=mesh['grp'=4,'seq'=32] {'seq'}, dimensions={0}, use_global_device_ids=true | all-gather | bytes 33792 | tf_op jit(solution)/shard_map/all_gather | solution.py:60
  166.8 4.5 %fusion.15 = (pred[256,8192]{0,1:T(8,128)(4,1)S(1)}, pred[]{:T(512)}) fusion(s32[256]{0:T(256)S(1)} %iota_add_fusion, s32[256]{0:T(256)S(1)} %copy-done.1, s32[8192]{0:T(1024)S(1)} %bitcast.82), kind=kLoop, calls=%fused_computation.18 | loop fusion | flops 8388607 | bytes 2131969 | tf_op jit(solution)/shard_map/and | solution.py:64
  172.0 0.1 slice_bitcast_fusion.6
  172.1 0.1 fusion.18
  172.2 1.0 fusion.17
  173.2 19.3 %all-gather.6.cloned.1.call-done = bf16[8192,2,128]{0,2,1:T(8,128)(2,1)} async-done(((bf16[256,2,128]{0,2,1:T(8,128)(2,1)}), bf16[8192,2,128]{0,2,1:T(8,128)(2,1)}) %all-gather.6.cloned.1.call-update) | async-done | bytes 4194320 | tf_op jit(solution)/shard_map/all_gather | solution.py:17
  192.5 77.8 %conditional.1 = (f32[1,8,256]{2,1,0:T(8,128)S(1)}, f32[1,8,256,128]{2,3,1,0:T(8,128)S(1)}) conditional(s32[]{:T(128)} %convert_element_type.50, () %tuple.13, (pred[256,8192]{0,1:T(8,128)(4,1)S(1)}, bf16[8192,2,128]{0,2,1:T(8,128)(2,1)}, bf16[256,1,8,128]{0,3,2,1:T(8,128)(2,1)}) %tuple.14), branch_computations={%region_1.0_spmd, %region_2.5_spmd} | conditional | flops 8808036352 | bytes 223920176 | solution.py:87
  192.5 6.4 %copy.24 = bf16[8192,2,128]{2,0,1:T(8,128)(2,1)} copy(bf16[8192,2,128]{0,2,1:T(8,128)(2,1)} %get-tuple-element.28) | data formatting | bytes 8388608 | tf_op jit(solution)/shard_map
  199.0 24.9 %fusion = (f32[8,256]{1,0:T(8,128)S(1)}, f32[8192,256,8]{1,0,2:T(8,128)}) fusion(pred[256,8192]{0,1:T(8,128)(4,1)S(1)} %get-tuple-element.14, bf16[256,1,8,128]{0,3,2,1:T(8,128)(2,1)S(1)} %copy-done, bf16[8192,2,128]{2,0,1:T(8,128)(2,1)} %copy.24), kind=kOutput, calls=%fused_computation.2 | convolution fusion | flops 4345296896 | bytes 71835648 | tf_op jit(solution)/shard_map/cond/branch_1_fun/qkgd,pkd->kgqp/dot_general | solution.py:72
  223.8 24.8 %fusion.8 = f32[1,8,256,128]{2,3,1,0:T(8,128)S(1)} fusion(bf16[8192,2,128]{2,0,1:T(8,128)(2,1)} %copy.24, f32[8192,256,8]{1,0,2:T(8,128)} %get-tuple-element.32, f32[8,256]{1,0:T(8,128)S(1)} %broadcast_maximum_fusion, pred[256,8192]{0,1:T(8,128)(4,1)S(1)} %get-tuple-element.14), kind=kOutput, calls=%fused_computation.11 | convolution fusion | flops 4378853376 | bytes 72359936 | tf_op jit(solution)/shard_map/cond/branch_1_fun/kgqp,pkd->kgqd/dot_general | solution.py:79
  248.7 21.7 %fusion.2 = f32[8,256]{1,0:T(8,128)S(1)} fusion(f32[8192,256,8]{1,0,2:T(8,128)} %get-tuple-element.32, f32[8,256]{1,0:T(8,128)S(1)} %broadcast_maximum_fusion, pred[256,8192]{0,1:T(8,128)(4,1)S(1)} %get-tuple-element.14), kind=kLoop, calls=%fused_computation.4 | loop fusion | flops 83884032 | bytes 69222400 | tf_op jit(solution)/shard_map/cond/branch_1_fun/reduce_sum | solution.py:78
  270.4 0.1 divide_convert_fusion
  270.5 12.7 %fusion.26 = f32[256,8192]{1,0:T(8,128)} fusion(bf16[256,1024]{0,1:T(8,128)(2,1)S(1)} %bitcast.81, bf16[1024,8192]{1,0:T(8,128)(2,1)} %param.10), kind=kOutput, calls=%fused_computation.47 | convolution fusion | flops 4294967296 | bytes 25690112 | tf_op jit(solution)/shard_map/dot_general | solution.py:91
  283.2 80.5 %reduce-scatter.2.cloned.1.call-done = f32[256,2048]{1,0:T(8,128)} async-done(((f32[256,8192]{1,0:T(8,128)}), f32[256,2048]{1,0:T(8,128)}) %reduce-scatter.2.cloned.1.call-update) | async-done | bytes 2097168 | tf_op jit(solution)/shard_map/reduce_scatter | solution.py:92
  363.8 2.7 convert_element_type.57
  (21 shorter events, 0.2 us)
Async XLA Ops:
  6.5 9.2 %copy-start.2 = (bf16[1280]{0:T(1024)(128)(2,1)S(1)}, bf16[1280]{0:T(1024)(128)(2,1)}, u32[]{:S(2)}) copy-start(bf16[1280]{0:T(1024)(128)(2,1)} %param.9) | copy-start | bytes 7684
  6.5 124.8 %all-gather.4.cloned.1.call-start = ((), (), s32[]{:S(2)}) async-start(), calls=%async_computation.2 | async-start | bytes 21626880 | tf_op jit(solution)/shard_map/all_gather | solution.py:40
  7.3 67.2 %all-to-all-start = ((bf16[32,256,256]{2,1,0:T(8,128)(2,1)}), bf16[32,256,256]{2,1,0:T(8,128)(2,1)}, u32[]{:S(2)}, u32[]{:S(2)}) async-start(bf16[32,256,256]{2,1,0:T(8,128)(2,1)} %bitcast.80), calls=%async_computation | async-start | bytes 8388608 | tf_op jit(solution)/shard_map/all_to_all | solution.py:37
  15.7 176.8 %all-gather.6.cloned.1.call-start = ((), (), s32[]{:S(2)}) async-start(), calls=%async_computation.3 | async-start | bytes 4325376 | tf_op jit(solution)/shard_map/all_gather | solution.py:17
  131.3 13.5 %copy-start.1 = (s32[256]{0:T(256)S(1)}, s32[256]{0:T(256)}, u32[]{:S(2)}) copy-start(s32[256]{0:T(256)} %param.11) | copy-start | bytes 3076
  144.7 219.0 %reduce-scatter.2.cloned.1.call-start = ((), (), s32[]{:S(2)}) async-start(), calls=%async_computation.4 | async-start | bytes 10485760 | tf_op jit(solution)/shard_map/reduce_scatter | solution.py:92
  192.5 6.4 %copy-start = (bf16[256,1,8,128]{0,3,2,1:T(8,128)(2,1)S(1)}, bf16[256,1,8,128]{0,3,2,1:T(8,128)(2,1)}, u32[]{:S(2)}) copy-start(bf16[256,1,8,128]{0,3,2,1:T(8,128)(2,1)} %get-tuple-element.29) | copy-start | bytes 1572868 | tf_op jit(solution)/shard_map/cond
Sparse Core Ops, SparseCore 0:
  9.6 121.6 all-gather.3
  144.9 47.6 all-gather.5
  283.3 80.3 reduce-scatter.1
where the time goes:
time: 375 us; the launch traced here: 373 us
  waiting for transfers between devices  209 us (56%)
  matrix products  74.6 us (20%)
  other arithmetic  31.1 us (8%)
  blocking collectives  22 us (6%)
  between operations  13.9 us (4%)
  local copies, waits for them, and re-layouts  13.4 us (4%)
  starting transfers between devices  8.52 us (2%)
    reduce_scatter x1, waiting for transfers between devices, body(): lax.psum_scatter(partial_value, 'grp', scatter_dimension=1, tiled=True)  80.5 us
    all_to_all x1, waiting for transfers between devices, body(): lax.all_to_all(tokens, 'seq', split_axis=0, concat_axis=1, tiled=True)  58.3 us
    all_gather x1, waiting for transfers between devices, body(): lax.all_gather(proj_weight, 'seq', axis=0, tiled=True)  50.4 us
    dot_general x1, matrix products, compute(): jnp.einsum('qkgd,pkd->kgqp', queries, key_block, preferred_element_type=j...  24.9 us
    dot_general x1, matrix products, compute(): jnp.einsum('kgqp,pkd->kgqd', weights.astype(jnp.bfloat16), value_block, p...  24.8 us
    all_gather x1, blocking collectives, body(): lax.all_gather(doc_ids, 'seq', axis=0, tiled=True)  22 us
    reduce_sum x1, other arithmetic, compute(): new_sum = jnp.sum(weights, axis=-1)  21.7 us
    all_gather x1, waiting for transfers between devices, in_one_piece(): filled = lax.all_gather(both, axis, axis=dim, tiled=True)  19.3 us
  transfers between devices with their start and end apart: 4, of which 4 were waited for; matrix products, arithmetic and copies ran while one was open for 3% of the time, Pallas kernels for 0%

commit v1 on v0

v1 whole, which is shorter than its diff:
```python
import functools
import jax
import jax.numpy as jnp
from jax import lax
from jax.experimental import pallas as pl
from jax.experimental.pallas import tpu as pltpu
from jax.sharding import Mesh, PartitionSpec as P

HEAD_DIM = 128
GQA = 8
TOK = 256
COLS = (GQA + 2) * HEAD_DIM
HALF = COLS // 2
BK = 512
theta_base = 1000000.0
NEG = -1e30
SCALE2 = HEAD_DIM ** -0.5 * 1.4426950408889634
BF = jnp.bfloat16
F32 = jnp.float32


def hop(x, axis, k, n=4):
    return lax.ppermute(x, axis, [(i, (i + k) % n) for i in range(n)])


def line_gather(x, axis):
    lo, hi, far = hop(x, axis, 1), hop(x, axis, -1), hop(x, axis, 2)
    return jnp.stack([x, lo, hi, far])


def plane_gather(a, b):
    la, lb = line_gather(a, "y"), line_gather(b, "z")
    am, ap = hop(la, "z", 1), hop(la, "z", -1)
    bm, bp = hop(lb, "y", 1), hop(lb, "y", -1)
    a0, a1 = hop(am[:2], "z", 1), hop(ap[2:], "z", -1)
    b0, b1 = hop(bm[:2], "y", 1), hop(bp[2:], "y", -1)
    return (la, am, ap, a0, a1), (lb, bm, bp, b0, b1)


def project_kernel(t0, t1, t2, t3, *refs, srcs):
    ws, out = refs[:-1], refs[-1]
    for n, (w, idx) in enumerate(zip(ws, srcs)):
        for m, s in enumerate(idx):
            lhs = jnp.concatenate([t0[s], t1[s], t2[s], t3[s]], axis=0)
            part = jnp.dot(lhs, w[m], preferred_element_type=F32)
            if n == 0 and m == 0:
                out[...] = part
            else:
                out[...] += part


def project(ts, ws, srcs):
    return pl.pallas_call(
        functools.partial(project_kernel, srcs=srcs),
        out_shape=jax.ShapeDtypeStruct((4 * 128, HALF), F32),
        name="project",
    )(*ts, *ws)


def rope(u, cos, sin):
    turned = jnp.concatenate([-u[:, HEAD_DIM // 2:], u[:, :HEAD_DIM // 2]], axis=1)
    return u * cos + turned * sin


def attend_kernel(
    info, q_in, q_got, bias, cos, sin, ids, *refs
):
    kv, (out, k_s, v_s, id_s, q_s, m_s, l_s, acc_s, sems) = refs[:20], refs[20:]
    y, z, c = info[0], info[1], info[2]
    offs = (0, -1, 1, 2)
    copies = []

    def place(src, row, dy, dz, core, which):
        by = lax.rem(y + dy + 4, 4)
        bz = lax.rem(z + dz + 4, 4)
        blk = by * 8 + bz * 2 + core
        dst = (k_s, v_s)[which]
        copies.append(pltpu.make_async_copy(
            src.at[row, pl.ds(0, TOK)], dst.at[pl.ds(pl.multiple_of(blk * TOK, TOK), TOK)], sems.at[which]))
        copies.append(pltpu.make_async_copy(
            src.at[row, pl.ds(TOK, 16)], id_s.at[which, pl.ds(pl.multiple_of(blk * 16, 16), 16)], sems.at[2 + which]))

    for side in range(2):
        core = c if side == 0 else 1 - c
        for which in range(2):
            group = kv[side * 10 + which * 5: side * 10 + which * 5 + 5]
            for arr, other, rows in zip(group, (0, -1, 1, 2, 2), (offs, offs, offs, offs[:2], offs[2:])):
                for r, o in enumerate(rows):
                    dy, dz = (o, other) if which == 0 else (other, o)
                    place(arr, r, dy, dz, core, which)
    for cp in copies:
        cp.start()
    cs, sn = cos[...], sin[...]
    for h in range(GQA):
        u = q_in[:, h * 128:(h + 1) * 128] + q_got[:, h * 128:(h + 1) * 128] + bias[:, h * 128:(h + 1) * 128].astype(F32)
        q_s[h * TOK:(h + 1) * TOK, :] = rope(u, cs, sn).astype(BF)
    m_s[...] = jnp.full_like(m_s, NEG)
    l_s[...] = jnp.zeros_like(l_s)
    acc_s[...] = jnp.zeros_like(acc_s)
    for cp in copies:
        cp.wait()
    rowsel = lax.rem(lax.broadcasted_iota(jnp.int32, (512, 128), 0), 16) == 0
    both = jnp.concatenate([id_s[0].astype(F32), id_s[1].astype(F32)], axis=1)
    sel2 = jnp.concatenate([rowsel, rowsel], axis=1)
    c1 = jnp.sum(jnp.where(sel2 & (both < 0.5), 1.0, 0.0)).astype(jnp.int32)
    c2 = jnp.sum(jnp.where(sel2 & (both < 1.5), 1.0, 0.0)).astype(jnp.int32)
    first = y * (8 * TOK) + z * (2 * TOK) + c * TOK
    mine = ids[...]
    start = jnp.where(mine == 0, 0, jnp.where(mine == 1, c1, c2))
    lo_start = jnp.where(first >= c2, c2, jnp.where(first >= c1, c1, 0))
    last = first + TOK - 1
    hi_start = jnp.where(last >= c2, c2, jnp.where(last >= c1, c1, 0))
    diag = first // BK
    lo = lo_start // BK
    full = jnp.minimum((hi_start + BK - 1) // BK, diag)
    pos = first + lax.broadcasted_iota(jnp.int32, (TOK, 1), 0)

    def block(j, masked, causal):
        base = pl.multiple_of(j * BK, BK)
        kb = k_s[pl.ds(base, BK), :]
        vb = v_s[pl.ds(base, BK), :]
        if masked or causal:
            kpos = base + lax.broadcasted_iota(jnp.int32, (TOK, BK), 1)
            ok = kpos >= start
            if causal:
                ok = ok & (kpos <= pos)
        for h in range(GQA):
            sl = pl.ds(h * TOK, TOK)
            s = lax.dot_general(q_s[sl, :], kb, (((1,), (1,)), ((), ())), preferred_element_type=F32)
            if masked or causal:
                s = jnp.where(ok, s, NEG)
            m_old = m_s[sl, :]
            m_new = jnp.maximum(m_old, jnp.max(s, axis=1, keepdims=True))
            p = jnp.exp2((s - m_new[:, :1]) * SCALE2)
            alpha = jnp.exp2((m_old - m_new) * SCALE2)
            m_s[sl, :] = m_new
            l_s[sl, :] = l_s[sl, :] * alpha + jnp.sum(p, axis=1, keepdims=True)
            acc_s[sl, :] = acc_s[sl, :] * alpha + jnp.dot(p.astype(BF), vb, preferred_element_type=F32)

    def loop(lo_, hi_, masked):
        def body_(j, carry):
            block(j, masked, False)
            return carry
        lax.fori_loop(lo_, hi_, body_, 0)

    loop(lo, full, True)
    loop(jnp.maximum(full, lo), diag, False)
    block(diag, True, True)
    for h in range(GQA):
        sl = pl.ds(h * TOK, TOK)
        out[:, h * 128:(h + 1) * 128] = (acc_s[sl, :] / l_s[sl, :]).astype(BF)


def attend(info, q_in, q_got, bias, cos, sin, ids, kv):
    vm = pl.BlockSpec(memory_space=pltpu.VMEM)
    hb = pl.BlockSpec(memory_space=pl.ANY)
    return pl.pallas_call(
        attend_kernel,
        out_shape=jax.ShapeDtypeStruct((TOK, GQA * HEAD_DIM), BF),
        in_specs=[pl.BlockSpec(memory_space=pltpu.SMEM)] + [vm] * 6 + [hb] * 20,
        out_specs=vm,
        scratch_shapes=[
            pltpu.VMEM((32 * TOK, HEAD_DIM), BF),
            pltpu.VMEM((32 * TOK, HEAD_DIM), BF),
            pltpu.VMEM((2, 32 * 16, HEAD_DIM), BF),
            pltpu.VMEM((GQA * TOK, HEAD_DIM), BF),
            pltpu.VMEM((GQA * TOK, HEAD_DIM), F32),
            pltpu.VMEM((GQA * TOK, HEAD_DIM), F32),
            pltpu.VMEM((GQA * TOK, HEAD_DIM), F32),
            pltpu.SemaphoreType.DMA((4,)),
        ],
        name="attend",
    )(info, q_in, q_got, bias, cos, sin, ids, *kv)


def kv_kernel(mine, got, bias, cos, sin, idrow, k_out, v_out):
    u = mine[...] + got[...] + bias[...].astype(F32)
    k_out[0:TOK, :] = rope(u[:, :HEAD_DIM], cos[...], sin[...]).astype(BF)
    v_out[0:TOK, :] = u[:, HEAD_DIM:].astype(BF)
    k_out[TOK:, :] = jnp.broadcast_to(idrow[0:1, :].astype(F32), (16, HEAD_DIM)).astype(BF)
    v_out[TOK:, :] = jnp.broadcast_to(idrow[1:2, :].astype(F32), (16, HEAD_DIM)).astype(BF)


def mix_kernel(blocks, a, w, o):
    o[...] = jnp.dot(a[...], w[...], preferred_element_type=F32).astype(o.dtype)


def mix(attended, out_weight, blocks, dtype):
    n = blocks.shape[0]
    return pl.pallas_call(
        mix_kernel,
        out_shape=jax.ShapeDtypeStruct((n, TOK, 1024), dtype),
        grid_spec=pltpu.PrefetchScalarGridSpec(
            num_scalar_prefetch=1,
            grid=(n,),
            in_specs=[
                pl.BlockSpec((TOK, 1024), lambda i, b: (0, 0)),
                pl.BlockSpec((1024, 1024), lambda i, b: (0, b[i])),
            ],
            out_specs=pl.BlockSpec((None, TOK, 1024), lambda i, b: (i, 0, 0)),
        ),
        name="mix",
    )(blocks, attended, out_weight)


def body(tokens, proj_weight, proj_bias, out_weight, doc_ids):
    x, y, z, c = (lax.axis_index(n) for n in ("grp", "y", "z", "c"))
    first = y * (8 * TOK) + z * (2 * TOK) + c * TOK
    quarter = lax.dynamic_slice(tokens.reshape(16, 4, 128, 256), (0, x, 0, 0), (16, 1, 128, 256)).reshape(16, 128, 256)
    got = lax.all_to_all(quarter, ("y", "z"), split_axis=0, concat_axis=0, tiled=True)
    wa, wb = plane_gather(proj_weight[:, :HALF], proj_weight[:, HALF:])
    got = got.reshape(4, 4, 128, 256)
    got = lax.dynamic_slice_in_dim(jnp.concatenate([got, got], axis=0), y, 4, axis=0)
    got = lax.dynamic_slice_in_dim(jnp.concatenate([got, got], axis=1), z, 4, axis=1)
    got = got.reshape(16, 128, 256)
    t_m, t_p = hop(got, "grp", 1), hop(got, "grp", -1)
    t_f = jnp.concatenate([hop(t_m[:8], "grp", 1), hop(t_p[8:], "grp", -1)], axis=0)
    ts = (got, t_p, t_f, t_m)
    offs = (0, 3, 1, 2)

    def halves(pieces, y_first):
        def src(o, other):
            return o * 4 + other if y_first else other * 4 + o
        near = [[src(o, d) for o in offs] for d in (0, 3, 1)]
        far = [[src(o, 2) for o in offs[:2]], [src(o, 2) for o in offs[2:]]]
        return project(ts, pieces[:3], near) + project(ts, pieces[3:], far)

    pa = halves(wa, True)
    pb = halves(wb, False)

    def rows(p, core):
        p = p.reshape(4, 128, p.shape[-1])
        return jnp.concatenate([
            lax.dynamic_index_in_dim(p, lax.rem(2 * core + j - x + 4, 4), 0, keepdims=False) for j in range(2)], axis=0)

    kv_part, q_part = pb[:, HALF - 256:], jnp.concatenate([pa, pb[:, :HALF - 256]], axis=1)
    kv_got = hop(rows(kv_part, 1 - c), "c", 1, 2)
    q_got = hop(rows(q_part, 1 - c), "c", 1, 2)
    bias = proj_bias.reshape(1, COLS)
    inverse_freq = theta_base ** (-(jnp.arange(HEAD_DIM // 2, dtype=F32) * 2.0) / HEAD_DIM)
    angles = (first + jnp.arange(TOK, dtype=jnp.int32)).astype(F32)[:, None] * inverse_freq[None, :]
    cos = jnp.concatenate([jnp.cos(angles), jnp.cos(angles)], axis=1)
    sin = jnp.concatenate([jnp.sin(angles), jnp.sin(angles)], axis=1)
    payload = jax.ShapeDtypeStruct((TOK + 16, HEAD_DIM), BF)
    k_own, v_own = pl.pallas_call(kv_kernel, out_shape=(payload, payload), name="kv")(
        rows(kv_part, c), kv_got, bias[:, 1024:], cos, sin, doc_ids.reshape(2, 128))
    k_all, v_all = plane_gather(k_own, v_own)
    mine = (*k_all, *v_all)
    other = tuple(hop(p, "c", 1, 2) for p in mine)
    info = jnp.stack([y, z, c]).astype(jnp.int32)
    attended = attend(info, rows(q_part, c), q_got, bias[:, :1024], cos, sin, doc_ids.reshape(TOK, 1), (*mine, *other))
    two = jnp.arange(2, dtype=jnp.int32)
    b_of = lambda d: lax.rem(x + d, 4).astype(jnp.int32) * 2 + two
    far = mix(attended, out_weight, b_of(2), BF)
    e_m, e_p = hop(far[0], "grp", 1), hop(far[1], "grp", -1)
    near = mix(attended, out_weight, jnp.concatenate([b_of(1), b_of(3), b_of(0)]), F32)
    to_p = jnp.concatenate([(near[0] + e_m.astype(F32)).astype(BF), near[1].astype(BF)], axis=1)
    to_m = jnp.concatenate([near[2].astype(BF), (near[3] + e_p.astype(F32)).astype(BF)], axis=1)
    r_m, r_p = hop(to_p, "grp", 1), hop(to_m, "grp", -1)
    own = jnp.concatenate([near[4], near[5]], axis=1)
    return (own + r_m.astype(F32) + r_p.astype(F32)).astype(BF)


def solution(mesh):
    fine = Mesh(mesh.devices.reshape(4, 4, 4, 2), ("grp", "y", "z", "c"))
    seq = ("y", "z", "c")
    return jax.shard_map(
        body,
        mesh=fine,
        in_specs=(P(None, seq), P(seq, "grp"), P("grp"), P("grp", None), P(seq)),
        out_specs=P(seq, "grp"),
        check_vma=False,
    )
```

time: 375 us -> 275 us (0.73)
  waiting for transfers between devices: 209 us -> 82.9 us
  Pallas kernels: 0 us -> 78.8 us
  matrix products: 74.6 us -> 0 us
  starting transfers between devices: 8.52 us -> 68.4 us
  blocking collectives: 22 us -> 0 us
  other arithmetic: 31.1 us -> 17.7 us
  between operations: 13.9 us -> 0.96 us
  local copies, waits for them, and re-layouts: 13.4 us -> 23.1 us
    reduce_scatter x1 -> x0, waiting for transfers between devices: 80.5 us -> none  [body(): lax.psum_scatter(partial_value, 'grp', scatter_dimension=1, tiled=True)]
    pallas_call x0 -> x8, Pallas kernels: none -> 78.8 us  [the longest x1 37.9 us: attend(): pl.pallas_call(attend_kernel, out_shape=jax.ShapeDtypeStruct((TOK, GQA *...]
    dot_general x4 -> x0, matrix products: 74.6 us -> none  [the longest x1 24.9 us: compute(): jnp.einsum('qkgd,pkd->kgqp', queries, key_block, preferred_element_type=j...]
    ppermute x0 -> x48, waiting for transfers between devices: none -> 71.3 us  [hop(): return lax.ppermute(x, axis, [(i, (i + k) % n) for i in range(n)])]
    all_gather x2 -> x0, waiting for transfers between devices: 69.7 us -> none  [the longest x1 50.4 us: body(): lax.all_gather(proj_weight, 'seq', axis=0, tiled=True)]
    ppermute x0 -> x48, starting transfers between devices: none -> 60.2 us  [hop(): return lax.ppermute(x, axis, [(i, (i + k) % n) for i in range(n)])]
    all_to_all x1, waiting for transfers between devices: 58.3 us -> 11.6 us  [body(): lax.all_to_all(quarter, ('y', 'z'), split_axis=0, concat_axis=0, tiled=True)]
    all_gather x1 -> x0, blocking collectives: 22 us -> none  [body(): lax.all_gather(doc_ids, 'seq', axis=0, tiled=True)]
  transfers between devices with their start and end apart: 4 -> 49, of which waited for: 4 -> 20; matrix products, arithmetic and copies ran while one was open for 3% -> 11% of each run, Pallas kernels for 0% -> 13%
where the time goes in v1:
time: 275 us; the launch traced here: 272 us
  waiting for transfers between devices  82.9 us (30%)
  Pallas kernels  78.8 us (29%)
  starting transfers between devices  68.4 us (25%)
  local copies, waits for them, and re-layouts  23.1 us (8%)
  other arithmetic  17.7 us (6%)
    ppermute x48, waiting for transfers between devices, hop(): return lax.ppermute(x, axis, [(i, (i + k) % n) for i in range(n)])  71.3 us
    ppermute x48, starting transfers between devices, hop(): return lax.ppermute(x, axis, [(i, (i + k) % n) for i in range(n)])  60.2 us
    pallas_call x1, Pallas kernels, attend(): pl.pallas_call(attend_kernel, out_shape=jax.ShapeDtypeStruct((TOK, GQA *...  37.9 us
    pallas_call x4, Pallas kernels, project(): pl.pallas_call(functools.partial(project_kernel, srcs=srcs), out_shape=ja...  23.5 us
    pallas_call x2, Pallas kernels, mix(): pl.pallas_call(mix_kernel, out_shape=jax.ShapeDtypeStruct((n, TOK, 1024),...  15.5 us
    all_to_all x1, waiting for transfers between devices, body(): lax.all_to_all(quarter, ('y', 'z'), split_axis=0, concat_axis=0, tiled=True)  11.6 us
    all_to_all x1, starting transfers between devices, body(): lax.all_to_all(quarter, ('y', 'z'), split_axis=0, concat_axis=0, tiled=True)  8.18 us
    unnamed x63, local copies, waits for them, and re-layouts  6.67 us
  transfers between devices with their start and end apart: 49, of which 20 were waited for; matrix products, arithmetic and copies ran while one was open for 11% of the time, Pallas kernels for 13%

profile of v1, /device:TPU:24, one launch (start us, length us, event | category | flops | bytes accessed | tf_op | source)
XLA Modules:
  0.0 271.9 jit_solution(143873922181227817)
XLA Ops:
  2.4 8.2 %all-to-all-start = ((bf16[16,128,256]{2,1,0:T(8,128)(2,1)}), bf16[16,128,256]{2,1,0:T(8,128)(2,1)S(1)}, u32[]{:S(2)}, u32[]{:S(2)}) async-start(bf16[16,128,256]{2,1,0:T(8,128)(2,1)} %dynamic-slice_bitcast_fusion), calls=%async_computation | async-start | bytes 2097152 | tf_op jit(solution)/shard_map/all_to_all | solution.py:210
  11.5 2.7 collective-permute-start.12
  14.2 11.6 %all-to-all-done = bf16[16,128,256]{2,1,0:T(8,128)(2,1)S(1)} async-done(((bf16[16,128,256]{2,1,0:T(8,128)(2,1)}), bf16[16,128,256]{2,1,0:T(8,128)(2,1)S(1)}, u32[]{:S(2)}, u32[]{:S(2)}) %all-to-all-start) | async-done | bytes 1048608 | tf_op jit(solution)/shard_map/all_to_all | solution.py:210
  31.4 6.2 %collective-permute-start.4 = (bf16[256,640]{1,0:T(8,128)(2,1)S(1)}, bf16[256,640]{1,0:T(8,128)(2,1)S(1)}, u32[]{:S(2)}, u32[]{:S(2)}) collective-permute-start(bf16[256,640]{1,0:T(8,128)(2,1)S(1)} %copy-done.21), channel_id=1, source_target_pairs={{0,8},{8,16},{16,24},{24,0},{1,9},{9,17},{17,25},{25,1},{2,10},{10... | collective-permute-start | bytes 983048 | tf_op jit(solution)/shard_map/ppermute | solution.py:23
  42.7 7.6 %collective-permute-done.4 = bf16[256,640]{1,0:T(8,128)(2,1)S(1)} collective-permute-done((bf16[256,640]{1,0:T(8,128)(2,1)S(1)}, bf16[256,640]{1,0:T(8,128)(2,1)S(1)}, u32[]{:S(2)}, u32[]{:S(2)}) %collective-permute-start.4) | collective-permute-done | bytes 327712 | tf_op jit(solution)/shard_map/ppermute | solution.py:23
  51.5 4.8 %collective-permute-start.8 = (bf16[4,256,640]{2,1,0:T(8,128)(2,1)}, bf16[4,256,640]{2,1,0:T(8,128)(2,1)S(1)}, u32[]{:S(2)}, u32[]{:S(2)}) collective-permute-start(bf16[4,256,640]{2,1,0:T(8,128)(2,1)} %pad_maximum_fusion.1.refs_0_), channel_id=1, source_target_pairs={{0,6},{2,0},{4,2},{6,4},{1,7},{3,1},{5,3},{7,5},{8,14},{10,8},{12,... | collective-permute-start | bytes 3932168 | tf_op jit(solution)/shard_map/ppermute | solution.py:23
  59.6 14.0 %collective-permute-done.15.refs_2_ = bf16[4,256,640]{2,1,0:T(8,128)(2,1)S(1)} collective-permute-done((bf16[4,256,640]{2,1,0:T(8,128)(2,1)S(1)}, bf16[4,256,640]{2,1,0:T(8,128)(2,1)S(1)}, u32[]{:S(2)}, u32[]{:S(2)}) %collective-permute-start.15) | collective-permute-done | bytes 1310752 | tf_op jit(solution)/shard_map/ppermute | solution.py:23
  77.3 3.5 %collective-permute-start.16 = (bf16[2,256,640]{2,1,0:T(8,128)(2,1)}, bf16[2,256,640]{2,1,0:T(8,128)(2,1)}, u32[]{:S(2)}, u32[]{:S(2)}) collective-permute-start(bf16[2,256,640]{2,1,0:T(8,128)(2,1)} %slice.102), channel_id=1, source_target_pairs={{0,8},{8,16},{16,24},{24,0},{1,9},{9,17},{17,25},{25,1},{2,10},{10... | collective-permute-start | bytes 1966088 | tf_op jit(solution)/shard_map/ppermute | solution.py:23
  82.7 2.8 %collective-permute-start.3 = (bf16[8,128,256]{2,1,0:T(8,128)(2,1)}, bf16[8,128,256]{2,1,0:T(8,128)(2,1)}, u32[]{:S(2)}, u32[]{:S(2)}) collective-permute-start(bf16[8,128,256]{2,1,0:T(8,128)(2,1)} %slice.99), channel_id=1, source_target_pairs={{0,96},{32,0},{64,32},{96,64},{1,97},{33,1},{65,33},{97,65},{2,98}... | collective-permute-start | bytes 1572872 | tf_op jit(solution)/shard_map/ppermute | solution.py:23
  86.6 3.7 %collective-permute-start.10 = (bf16[2,256,640]{2,1,0:T(8,128)(2,1)S(1)}, bf16[2,256,640]{2,1,0:T(8,128)(2,1)}, u32[]{:S(2)}, u32[]{:S(2)}) collective-permute-start(bf16[2,256,640]{2,1,0:T(8,128)(2,1)S(1)} %slice.101), channel_id=1, source_target_pairs={{0,6},{2,0},{4,2},{6,4},{1,7},{3,1},{5,3},{7,5},{8,14},{10,8},{12,... | collective-permute-start | bytes 1966088 | tf_op jit(solution)/shard_map/ppermute | solution.py:23
  97.3 7.0 %project.6 = f32[512,640]{1,0:T(8,128)} custom-call(bf16[16,128,256]{2,1,0:T(8,128)(2,1)} %bitcast.72, bf16[16,128,256]{2,1,0:T(8,128)(2,1)} %copy-done.3, bf16[16,128,256]{2,1,0:T(8,128)(2,1)} %copy-done.4, bf16[16,128,256]{2,1,0:T(8,128)(2,1)} %copy-done.2, bf16[4,256,640]{2,1,0:T(8,128)(2,1)} %copy-done.5, bf16[4,256,640]{2,1,0:T(8,128)(2,1)} %copy-done.11, ...), custom_call_target="tpu_custom_call" | custom-call | tf_op jit(solution)/shard_map/project/pallas_call | solution.py:53
  104.3 4.7 %project.7 = f32[512,640]{1,0:T(8,128)} custom-call(bf16[16,128,256]{2,1,0:T(8,128)(2,1)} %bitcast.73, bf16[16,128,256]{2,1,0:T(8,128)(2,1)} %copy-done.3, bf16[16,128,256]{2,1,0:T(8,128)(2,1)} %copy-done.4, bf16[16,128,256]{2,1,0:T(8,128)(2,1)} %copy-done.2, bf16[2,256,640]{2,1,0:T(8,128)(2,1)} %collective-permute-done.16.refs_0_, ...), custom_call_target="tpu_custom_call" | custom-call | tf_op jit(solution)/shard_map/project/pallas_call | solution.py:53
  114.1 7.0 %project.4 = f32[512,640]{1,0:T(8,128)} custom-call(bf16[16,128,256]{2,1,0:T(8,128)(2,1)} %bitcast.74, bf16[16,128,256]{2,1,0:T(8,128)(2,1)} %copy-done.3, bf16[16,128,256]{2,1,0:T(8,128)(2,1)} %copy-done.4, bf16[16,128,256]{2,1,0:T(8,128)(2,1)} %copy-done.2, bf16[4,256,640]{2,1,0:T(8,128)(2,1)} %pad_maximum_fusion.1.refs_0_, ...), custom_call_target="tpu_custom_call" | custom-call | tf_op jit(solution)/shard_map/project/pallas_call | solution.py:53
  121.2 4.7 %project.5 = f32[512,640]{1,0:T(8,128)} custom-call(bf16[16,128,256]{2,1,0:T(8,128)(2,1)} %bitcast.75, bf16[16,128,256]{2,1,0:T(8,128)(2,1)} %copy-done.3, bf16[16,128,256]{2,1,0:T(8,128)(2,1)} %copy-done.4, bf16[16,128,256]{2,1,0:T(8,128)(2,1)} %copy-done.2, bf16[2,256,640]{2,1,0:T(8,128)(2,1)} %collective-permute-done.9.refs_0_, ...), custom_call_target="tpu_custom_call" | custom-call | tf_op jit(solution)/shard_map/project/pallas_call | solution.py:53
  140.3 3.1 %collective-permute-start.22 = (bf16[272,128]{1,0:T(8,128)(2,1)S(1)}, bf16[272,128]{1,0:T(8,128)(2,1)S(1)}, u32[]{:S(2)}, u32[]{:S(2)}) collective-permute-start(bf16[272,128]{1,0:T(8,128)(2,1)S(1)} %copy-done.27), channel_id=1, source_target_pairs={{0,16},{8,24},{16,0},{24,8},{1,17},{9,25},{17,1},{25,9},{2,18},{10... | collective-permute-start | bytes 208904 | tf_op jit(solution)/shard_map/ppermute | solution.py:23
  154.5 3.1 %collective-permute-start.32 = (bf16[2,272,128]{2,1,0:T(8,128)(2,1)S(1)}, bf16[2,272,128]{2,1,0:T(8,128)(2,1)S(1)}, u32[]{:S(2)}, u32[]{:S(2)}) collective-permute-start(bf16[2,272,128]{2,1,0:T(8,128)(2,1)S(1)} %slice.110), channel_id=1, source_target_pairs={{0,8},{8,16},{16,24},{24,0},{1,9},{9,17},{17,25},{25,1},{2,10},{10... | collective-permute-start | bytes 417800 | tf_op jit(solution)/shard_map/ppermute | solution.py:23
  160.3 3.0 %collective-permute-done.23.refs_1_ = bf16[4,272,128]{2,1,0:T(8,128)(2,1)S(1)} collective-permute-done((bf16[4,272,128]{2,1,0:T(8,128)(2,1)S(1)}, bf16[4,272,128]{2,1,0:T(8,128)(2,1)S(1)}, u32[]{:S(2)}, u32[]{:S(2)}) %collective-permute-start.23) | collective-permute-done | bytes 278560 | tf_op jit(solution)/shard_map/ppermute | solution.py:23
  177.8 37.9 %attend.1.a = bf16[256,1024]{1,0:T(8,128)(2,1)} custom-call(s32[3]{0:T(128)} %pad_add_fusion.1.info, f32[256,1024]{1,0:T(8,128)} %pad_maximum_fusion.3.q_in, f32[256,1024]{1,0:T(8,128)} %copy-done.14, bf16[1,1024]{1,0:T(2,128)(2,1)} %slice.105.bias, f32[256,128]{1,0:T(8,128)} %get-tuple-element.33.cos, f32[256,128]{1,0:T(8,128)} %get-tuple-element.34.sin, ...), custom_call_target="tpu_custom_call" | custom-call | tf_op jit(solution)/shard_map/attend/pallas_call | solution.py:157
  215.8 4.6 %mix.3 = bf16[2,256,1024]{2,1,0:T(8,128)(2,1)} custom-call(s32[2]{0:T(128)} %iota_add_fusion.blocks, bf16[256,1024]{1,0:T(8,128)(2,1)} %attend.1.a, bf16[1024,8192]{1,0:T(8,128)(2,1)} %w.3), custom_call_target="tpu_custom_call" | custom-call | tf_op jit(solution)/shard_map/mix/pallas_call | solution.py:190
  222.5 3.0 %collective-permute-start.46 = (bf16[256,1024]{1,0:T(8,128)(2,1)S(1)}, bf16[256,1024]{1,0:T(8,128)(2,1)S(1)}, u32[]{:S(2)}, u32[]{:S(2)}) collective-permute-start(bf16[256,1024]{1,0:T(8,128)(2,1)S(1)} %get-tuple-element.20), channel_id=1, source_target_pairs={{0,96},{32,0},{64,32},{96,64},{1,97},{33,1},{65,33},{97,65},{2,98}... | collective-permute-start | bytes 1572872 | tf_op jit(solution)/shard_map/ppermute | solution.py:23
  226.1 10.9 %mix.2 = f32[6,256,1024]{2,1,0:T(8,128)} custom-call(s32[6]{0:T(128)} %pad_add_fusion.blocks, bf16[256,1024]{1,0:T(8,128)(2,1)} %attend.1.a, bf16[1024,8192]{1,0:T(8,128)(2,1)} %w.3), custom_call_target="tpu_custom_call" | custom-call | tf_op jit(solution)/shard_map/mix/pallas_call | solution.py:190
  237.0 3.4 %convert.4 = bf16[6,256,1024]{2,1,0:T(8,128)(2,1)S(1)} convert(f32[6,256,1024]{2,1,0:T(8,128)} %mix.2) | non-fusion elementwise | flops 1572864 | bytes 9437184 | tf_op jit(solution)/shard_map/convert.1
  244.5 22.8 %collective-permute-done.47 = bf16[256,2048]{1,0:T(8,128)(2,1)S(1)} collective-permute-done((bf16[256,2048]{1,0:T(8,128)(2,1)S(1)}, bf16[256,2048]{1,0:T(8,128)(2,1)S(1)}, u32[]{:S(2)}, u32[]{:S(2)}) %collective-permute-start.47) | collective-permute-done | bytes 1048608 | tf_op jit(solution)/shard_map/ppermute | solution.py:23
  267.3 2.7 %collective-permute-done.45 = bf16[256,2048]{1,0:T(8,128)(2,1)S(1)} collective-permute-done((bf16[256,2048]{1,0:T(8,128)(2,1)S(1)}, bf16[256,2048]{1,0:T(8,128)(2,1)S(1)}, u32[]{:S(2)}, u32[]{:S(2)}) %collective-permute-start.45) | collective-permute-done | bytes 1048608 | tf_op jit(solution)/shard_map/ppermute | solution.py:23
  (197 shorter events, 87.8 us)
Async XLA Ops:
  2.4 23.4 %all-to-all-start = ((bf16[16,128,256]{2,1,0:T(8,128)(2,1)}), bf16[16,128,256]{2,1,0:T(8,128)(2,1)S(1)}, u32[]{:S(2)}, u32[]{:S(2)}) async-start(bf16[16,128,256]{2,1,0:T(8,128)(2,1)} %dynamic-slice_bitcast_fusion), calls=%async_computation | async-start | bytes 2097152 | tf_op jit(solution)/shard_map/all_to_all | solution.py:210
  11.5 19.9 %collective-permute-start.12 = (bf16[256,640]{1,0:T(8,128)(2,1)}, bf16[256,640]{1,0:T(8,128)(2,1)S(1)}, u32[]{:S(2)}, u32[]{:S(2)}) collective-permute-start(bf16[256,640]{1,0:T(8,128)(2,1)} %get-tuple-element.23), channel_id=1, source_target_pairs={{0,6},{2,0},{4,2},{6,4},{1,7},{3,1},{5,3},{7,5},{8,14},{10,8},{12,... | collective-permute-start | bytes 983048 | tf_op jit(solution)/shard_map/ppermute | solution.py:23
  14.2 23.5 %collective-permute-start.11 = (bf16[256,640]{1,0:T(8,128)(2,1)}, bf16[256,640]{1,0:T(8,128)(2,1)S(1)}, u32[]{:S(2)}, u32[]{:S(2)}) collective-permute-start(bf16[256,640]{1,0:T(8,128)(2,1)} %get-tuple-element.23), channel_id=1, source_target_pairs={{0,2},{2,4},{4,6},{6,0},{1,3},{3,5},{5,7},{7,1},{8,10},{10,12},{12... | collective-permute-start | bytes 983048 | tf_op jit(solution)/shard_map/ppermute | solution.py:23
  26.6 32.2 %collective-permute-start.1 = (bf16[16,128,256]{2,1,0:T(8,128)(2,1)S(1)}, bf16[16,128,256]{2,1,0:T(8,128)(2,1)S(1)}, u32[]{:S(2)}, u32[]{:S(2)}) collective-permute-start(bf16[16,128,256]{2,1,0:T(8,128)(2,1)S(1)} %bitcast.70), channel_id=1, source_target_pairs={{0,32},{32,64},{64,96},{96,0},{1,33},{33,65},{65,97},{97,1},{2,34}... | collective-permute-start | bytes 3145736 | tf_op jit(solution)/shard_map/ppermute | solution.py:23
  31.4 18.8 %collective-permute-start.4 = (bf16[256,640]{1,0:T(8,128)(2,1)S(1)}, bf16[256,640]{1,0:T(8,128)(2,1)S(1)}, u32[]{:S(2)}, u32[]{:S(2)}) collective-permute-start(bf16[256,640]{1,0:T(8,128)(2,1)S(1)} %copy-done.21), channel_id=1, source_target_pairs={{0,8},{8,16},{16,24},{24,0},{1,9},{9,17},{17,25},{25,1},{2,10},{10... | collective-permute-start | bytes 983048 | tf_op jit(solution)/shard_map/ppermute | solution.py:23
  37.6 12.6 %collective-permute-start.6 = (bf16[256,640]{1,0:T(8,128)(2,1)S(1)}, bf16[256,640]{1,0:T(8,128)(2,1)S(1)}, u32[]{:S(2)}, u32[]{:S(2)}) collective-permute-start(bf16[256,640]{1,0:T(8,128)(2,1)S(1)} %copy-done.21), channel_id=1, source_target_pairs={{0,16},{8,24},{16,0},{24,8},{1,17},{9,25},{17,1},{25,9},{2,18},{10... | collective-permute-start | bytes 983048 | tf_op jit(solution)/shard_map/ppermute | solution.py:23
  39.4 34.3 %collective-permute-start.15 = (bf16[4,256,640]{2,1,0:T(8,128)(2,1)S(1)}, bf16[4,256,640]{2,1,0:T(8,128)(2,1)S(1)}, u32[]{:S(2)}, u32[]{:S(2)}) collective-permute-start(bf16[4,256,640]{2,1,0:T(8,128)(2,1)S(1)} %pad_maximum_fusion.2.refs_0_), channel_id=1, source_target_pairs={{0,24},{8,0},{16,8},{24,16},{1,25},{9,1},{17,9},{25,17},{2,26},{10... | collective-permute-start | bytes 3932168 | tf_op jit(solution)/shard_map/ppermute | solution.py:23
  40.8 35.3 %collective-permute-start.14 = (bf16[4,256,640]{2,1,0:T(8,128)(2,1)S(1)}, bf16[4,256,640]{2,1,0:T(8,128)(2,1)S(1)}, u32[]{:S(2)}, u32[]{:S(2)}) collective-permute-start(bf16[4,256,640]{2,1,0:T(8,128)(2,1)S(1)} %pad_maximum_fusion.2.refs_0_), channel_id=1, source_target_pairs={{0,8},{8,16},{16,24},{24,0},{1,9},{9,17},{17,25},{25,1},{2,10},{10... | collective-permute-start | bytes 3932168 | tf_op jit(solution)/shard_map/ppermute | solution.py:23
  51.5 30.1 %collective-permute-start.8 = (bf16[4,256,640]{2,1,0:T(8,128)(2,1)}, bf16[4,256,640]{2,1,0:T(8,128)(2,1)S(1)}, u32[]{:S(2)}, u32[]{:S(2)}) collective-permute-start(bf16[4,256,640]{2,1,0:T(8,128)(2,1)} %pad_maximum_fusion.1.refs_0_), channel_id=1, source_target_pairs={{0,6},{2,0},{4,2},{6,4},{1,7},{3,1},{5,3},{7,5},{8,14},{10,8},{12,... | collective-permute-start | bytes 3932168 | tf_op jit(solution)/shard_map/ppermute | solution.py:23
  56.3 21.0 %collective-permute-start = (bf16[16,128,256]{2,1,0:T(8,128)(2,1)S(1)}, bf16[16,128,256]{2,1,0:T(8,128)(2,1)S(1)}, u32[]{:S(2)}, u32[]{:S(2)}) collective-permute-start(bf16[16,128,256]{2,1,0:T(8,128)(2,1)S(1)} %bitcast.71), channel_id=1, source_target_pairs={{0,96},{32,0},{64,32},{96,64},{1,97},{33,1},{65,33},{97,65},{2,98}... | collective-permute-start | bytes 3145736 | tf_op jit(solution)/shard_map/ppermute | solution.py:23
  58.7 27.9 %collective-permute-start.7 = (bf16[4,256,640]{2,1,0:T(8,128)(2,1)}, bf16[4,256,640]{2,1,0:T(8,128)(2,1)}, u32[]{:S(2)}, u32[]{:S(2)}) collective-permute-start(bf16[4,256,640]{2,1,0:T(8,128)(2,1)} %pad_maximum_fusion.1.refs_0_), channel_id=1, source_target_pairs={{0,2},{2,4},{4,6},{6,0},{1,3},{3,5},{5,7},{7,1},{8,10},{10,12},{12... | collective-permute-start | bytes 3932168 | tf_op jit(solution)/shard_map/ppermute | solution.py:23
  73.7 18.6 %collective-permute-start.2 = (bf16[8,128,256]{2,1,0:T(8,128)(2,1)}, bf16[8,128,256]{2,1,0:T(8,128)(2,1)}, u32[]{:S(2)}, u32[]{:S(2)}) collective-permute-start(bf16[8,128,256]{2,1,0:T(8,128)(2,1)} %slice.98), channel_id=1, source_target_pairs={{0,32},{32,64},{64,96},{96,0},{1,33},{33,65},{65,97},{97,1},{2,34}... | collective-permute-start | bytes 1572872 | tf_op jit(solution)/shard_map/ppermute | solution.py:23
  76.1 28.2 %collective-permute-start.17 = (bf16[2,256,640]{2,1,0:T(8,128)(2,1)}, bf16[2,256,640]{2,1,0:T(8,128)(2,1)}, u32[]{:S(2)}, u32[]{:S(2)}) collective-permute-start(bf16[2,256,640]{2,1,0:T(8,128)(2,1)} %slice.103), channel_id=1, source_target_pairs={{0,24},{8,0},{16,8},{24,16},{1,25},{9,1},{17,9},{25,17},{2,26},{10... | collective-permute-start | bytes 1966088 | tf_op jit(solution)/shard_map/ppermute | solution.py:23
  77.3 27.1 %collective-permute-start.16 = (bf16[2,256,640]{2,1,0:T(8,128)(2,1)}, bf16[2,256,640]{2,1,0:T(8,128)(2,1)}, u32[]{:S(2)}, u32[]{:S(2)}) collective-permute-start(bf16[2,256,640]{2,1,0:T(8,128)(2,1)} %slice.102), channel_id=1, source_target_pairs={{0,8},{8,16},{16,24},{24,0},{1,9},{9,17},{17,25},{25,1},{2,10},{10... | collective-permute-start | bytes 1966088 | tf_op jit(solution)/shard_map/ppermute | solution.py:23
  82.7 12.5 %collective-permute-start.3 = (bf16[8,128,256]{2,1,0:T(8,128)(2,1)}, bf16[8,128,256]{2,1,0:T(8,128)(2,1)}, u32[]{:S(2)}, u32[]{:S(2)}) collective-permute-start(bf16[8,128,256]{2,1,0:T(8,128)(2,1)} %slice.99), channel_id=1, source_target_pairs={{0,96},{32,0},{64,32},{96,64},{1,97},{33,1},{65,33},{97,65},{2,98}... | collective-permute-start | bytes 1572872 | tf_op jit(solution)/shard_map/ppermute | solution.py:23
  86.6 34.6 %collective-permute-start.10 = (bf16[2,256,640]{2,1,0:T(8,128)(2,1)S(1)}, bf16[2,256,640]{2,1,0:T(8,128)(2,1)}, u32[]{:S(2)}, u32[]{:S(2)}) collective-permute-start(bf16[2,256,640]{2,1,0:T(8,128)(2,1)S(1)} %slice.101), channel_id=1, source_target_pairs={{0,6},{2,0},{4,2},{6,4},{1,7},{3,1},{5,3},{7,5},{8,14},{10,8},{12,... | collective-permute-start | bytes 1966088 | tf_op jit(solution)/shard_map/ppermute | solution.py:23
  92.3 28.9 %collective-permute-start.9 = (bf16[2,256,640]{2,1,0:T(8,128)(2,1)}, bf16[2,256,640]{2,1,0:T(8,128)(2,1)}, u32[]{:S(2)}, u32[]{:S(2)}) collective-permute-start(bf16[2,256,640]{2,1,0:T(8,128)(2,1)} %slice.100), channel_id=1, source_target_pairs={{0,2},{2,4},{4,6},{6,0},{1,3},{3,5},{5,7},{7,1},{8,10},{10,12},{12... | collective-permute-start | bytes 1966088 | tf_op jit(solution)/shard_map/ppermute | solution.py:23
  112.2 16.0 %collective-permute-start.19 = (f32[256,256]{1,0:T(8,128)}, f32[256,256]{1,0:T(8,128)}, u32[]{:S(2)}, u32[]{:S(2)}) collective-permute-start(f32[256,256]{1,0:T(8,128)} %pad_maximum_fusion.10), channel_id=1, source_target_pairs={{0,1},{1,0},{2,3},{3,2},{4,5},{5,4},{6,7},{7,6},{8,9},{9,8},{10,11... | collective-permute-start | bytes 786440 | tf_op jit(solution)/shard_map/ppermute | solution.py:23
  139.3 12.3 %collective-permute-start.31 = (bf16[4,272,128]{2,1,0:T(8,128)(2,1)S(1)}, bf16[4,272,128]{2,1,0:T(8,128)(2,1)S(1)}, u32[]{:S(2)}, u32[]{:S(2)}) collective-permute-start(bf16[4,272,128]{2,1,0:T(8,128)(2,1)S(1)} %pad_maximum_fusion.8.refs_5_), channel_id=1, source_target_pairs={{0,24},{8,0},{16,8},{24,16},{1,25},{9,1},{17,9},{25,17},{2,26},{10... | collective-permute-start | bytes 835592 | tf_op jit(solution)/shard_map/ppermute | solution.py:23
  150.2 26.6 %collective-permute-start.18 = (f32[256,1024]{1,0:T(8,128)}, f32[256,1024]{1,0:T(8,128)S(1)}, u32[]{:S(2)}, u32[]{:S(2)}) collective-permute-start(f32[256,1024]{1,0:T(8,128)} %pad_maximum_fusion.4), channel_id=1, source_target_pairs={{0,1},{1,0},{2,3},{3,2},{4,5},{5,4},{6,7},{7,6},{8,9},{9,8},{10,11... | collective-permute-start | bytes 3145736 | tf_op jit(solution)/shard_map/ppermute | solution.py:23
  221.6 18.9 %collective-permute-start.44 = (bf16[256,1024]{1,0:T(8,128)(2,1)S(1)}, bf16[256,1024]{1,0:T(8,128)(2,1)S(1)}, u32[]{:S(2)}, u32[]{:S(2)}) collective-permute-start(bf16[256,1024]{1,0:T(8,128)(2,1)S(1)} %get-tuple-element.19), channel_id=1, source_target_pairs={{0,32},{32,64},{64,96},{96,0},{1,33},{33,65},{65,97},{97,1},{2,34}... | collective-permute-start | bytes 1572872 | tf_op jit(solution)/shard_map/ppermute | solution.py:23
  222.5 18.1 %collective-permute-start.46 = (bf16[256,1024]{1,0:T(8,128)(2,1)S(1)}, bf16[256,1024]{1,0:T(8,128)(2,1)S(1)}, u32[]{:S(2)}, u32[]{:S(2)}) collective-permute-start(bf16[256,1024]{1,0:T(8,128)(2,1)S(1)} %get-tuple-element.20), channel_id=1, source_target_pairs={{0,96},{32,0},{64,32},{96,64},{1,97},{33,1},{65,33},{97,65},{2,98}... | collective-permute-start | bytes 1572872 | tf_op jit(solution)/shard_map/ppermute | solution.py:23
  242.1 25.2 %collective-permute-start.47 = (bf16[256,2048]{1,0:T(8,128)(2,1)S(1)}, bf16[256,2048]{1,0:T(8,128)(2,1)S(1)}, u32[]{:S(2)}, u32[]{:S(2)}) collective-permute-start(bf16[256,2048]{1,0:T(8,128)(2,1)S(1)} %pad_maximum_fusion.6), channel_id=1, source_target_pairs={{0,96},{32,0},{64,32},{96,64},{1,97},{33,1},{65,33},{97,65},{2,98}... | collective-permute-start | bytes 3145736 | tf_op jit(solution)/shard_map/ppermute | solution.py:23
  244.2 25.8 %collective-permute-start.45 = (bf16[256,2048]{1,0:T(8,128)(2,1)S(1)}, bf16[256,2048]{1,0:T(8,128)(2,1)S(1)}, u32[]{:S(2)}, u32[]{:S(2)}) collective-permute-start(bf16[256,2048]{1,0:T(8,128)(2,1)S(1)} %pad_maximum_fusion.5), channel_id=1, source_target_pairs={{0,32},{32,64},{64,96},{96,0},{1,33},{33,65},{65,97},{97,1},{2,34}... | collective-permute-start | bytes 3145736 | tf_op jit(solution)/shard_map/ppermute | solution.py:23
  (57 other events, 522.6 us)

commit v2 on v1

v2 whole, which is shorter than its diff:
```python
import functools
import jax
import jax.numpy as jnp
from jax import lax
from jax.experimental import pallas as pl
from jax.experimental.pallas import tpu as pltpu
from jax.sharding import Mesh, PartitionSpec as P


HEAD_DIM = 128
GQA = 8
TOK = 256
COLS = (GQA + 2) * HEAD_DIM
BK = 512
PAY = 2 * TOK + 16
OFFS = (0, 3, 1, 2)
theta_base = 1000000.0
NEG = -1e30
SCALE2 = HEAD_DIM ** -0.5 * 1.4426950408889634
BF = jnp.bfloat16
F32 = jnp.float32


def hop(x, axis, k, n=4):
    return lax.ppermute(x, axis, [(i, (i + k) % n) for i in range(n)])


def swap(x):
    return hop(x, "c", 1, 2)


def turn(x, k, second):
    pairs = []
    for y in range(4):
        for z in range(4):
            for c in range(2):
                along_y = (c == 0) != second
                to = ((y + k) % 4, z) if along_y else (y, (z + k) % 4)
                pairs.append((y * 8 + z * 2 + c, to[0] * 8 + to[1] * 2 + c))
    return lax.ppermute(x, ("y", "z", "c"), pairs)


def line_gather(x):
    return jnp.stack([x, turn(x, 1, False), turn(x, -1, False), turn(x, 2, False)])


def plane_gather(w):
    lo, hi = jnp.stack([w, turn(w, 1, False)]), jnp.stack([turn(w, -1, False), turn(w, 2, False)])
    lo, hi = lax.optimization_barrier((lo, hi))
    near = [turn(v, k, True) for k in (1, -1) for v in (lo, hi)]
    m_lo, m_hi, p_lo, p_hi = lax.optimization_barrier(tuple(near))
    f_lo, f_hi = turn(m_lo, 1, True), turn(p_hi, -1, True)
    return (lo, hi, m_lo, m_hi, p_lo, p_hi), (f_lo, f_hi)


def gather_rows(t, d):
    return jnp.concatenate([jnp.concatenate(
        [t[2 * k + n // 2][n % 2, d] for k in range(4)], axis=0) for n in range(4)], axis=1)


def token_specs(d):
    n, at = (4, 0) if d is None else (1, d)
    return [pl.BlockSpec((2, n, 128, 256), lambda i, *_: (0, at, 0, 0))] * 8


def near_kernel(*refs):
    t, ws, (out, lhs) = refs[:8], refs[8:14], refs[14:]

    @pl.when(pl.program_id(0) == 0)
    def _():
        for n, d in enumerate(OFFS[:3]):
            lhs[:, n * 1024:(n + 1) * 1024] = gather_rows(t, d)

    rhs = jnp.concatenate([w[...].reshape(512, 256) for w in ws], axis=0)
    out[...] = jnp.dot(lhs[...], rhs, preferred_element_type=F32)


def near_project(ts, ws):
    return pl.pallas_call(
        near_kernel,
        out_shape=jax.ShapeDtypeStruct((512, COLS), F32),
        grid=(5,),
        in_specs=token_specs(None) + [pl.BlockSpec((2, 256, 256), lambda i: (0, 0, i))] * 6,
        out_specs=pl.BlockSpec((512, 256), lambda i: (0, i)),
        scratch_shapes=[pltpu.VMEM((512, 3072), BF)],
        cost_estimate=pl.CostEstimate(flops=2 * 512 * 3072 * COLS, bytes_accessed=14 << 20, transcendentals=0),
        name="near",
    )(*ts, *ws)


def far_kernel(info, *refs, kv):
    t, (w0, w1, acc, mine, other, tot) = refs[:8], refs[8:]
    lhs = gather_rows(t, 0)
    rhs = jnp.concatenate([w0[...].reshape(512, 256), w1[...].reshape(512, 256)], axis=0)
    tot[...] = acc[...] + jnp.dot(lhs, rhs, preferred_element_type=F32)
    for b in range(4):
        k = lax.rem(b - info[0] + 4, 4)
        row = pl.ds(pl.multiple_of(k * 128, 128), 128)
        if kv:
            keys, values = tot[row, :128], tot[row, 128:]
            first = info[3] == 0
            mine[b * 128:(b + 1) * 128, :] = jnp.where(first, keys, values)
            other[b * 128:(b + 1) * 128, :] = jnp.where(first, values, keys)
        else:
            got = tot[row, :]
            at = slice((b % 2) * 128, (b % 2) * 128 + 128)

            @pl.when(info[3] == b // 2)
            def _(got=got, at=at):
                mine[at, :] = got

            @pl.when(info[3] != b // 2)
            def _(got=got, at=at):
                other[at, :] = got


def far_project(info, ts, ws, acc, kv):
    steps, base = (1, 4) if kv else (4, 0)
    half = jax.ShapeDtypeStruct((512, 128) if kv else (256, 1024), F32)
    ospec = pl.BlockSpec((512, 128) if kv else (256, 256), lambda i, _: (0, i))
    piece = pl.BlockSpec((2, 256, 256), lambda i, _: (0, 0, i + base))
    return pl.pallas_call(
        functools.partial(far_kernel, kv=kv),
        out_shape=(half, half),
        grid_spec=pltpu.PrefetchScalarGridSpec(
            num_scalar_prefetch=1,
            grid=(steps,),
            in_specs=token_specs(2) + [piece, piece, pl.BlockSpec((512, 256), lambda i, _: (0, i + base))],
            out_specs=(ospec, ospec),
            scratch_shapes=[pltpu.VMEM((512, 256), F32)],
        ),
        cost_estimate=pl.CostEstimate(flops=2 * 512 * 1024 * 256 * steps, bytes_accessed=5 << 20, transcendentals=0),
        name="far_kv" if kv else "far_q",
    )(info, *ts, *ws, acc)


def rope(u, cos, sin):
    turned = jnp.concatenate([-u[:, HEAD_DIM // 2:], u[:, :HEAD_DIM // 2]], axis=1)
    return u * cos + turned * sin


def attend_kernel(info, q_in, q_got, bias, cos, sin, ids, *refs):
    kv, (out, kv_s, q_s, m_s, l_s, acc_s, sems) = refs[:8], refs[8:]
    y, z, c = info[1], info[2], info[3]
    copies = []
    for side in range(2):
        kind = c if side == 0 else 1 - c
        for d, arr in zip(OFFS, kv[side * 4:side * 4 + 4]):
            for r, o in enumerate(OFFS):
                by = lax.rem(y + jnp.where(kind == 0, o, d), 4)
                bz = lax.rem(z + jnp.where(kind == 0, d, o), 4)
                copies.append(pltpu.make_async_copy(arr.at[r], kv_s.at[kind, by * 4 + bz], sems.at[side]))
    for cp in copies:
        cp.start()
    cs, sn = cos[...] * SCALE2, sin[...] * SCALE2
    for h in range(GQA):
        col = slice(h * 128, h * 128 + 128)
        u = q_in[:, col] + q_got[:, col] + bias[:, col].astype(F32)
        q_s[h] = rope(u, cs, sn).astype(BF)
    m_s[...] = jnp.full_like(m_s, NEG)
    l_s[...] = jnp.zeros_like(l_s)
    acc_s[...] = jnp.zeros_like(acc_s)
    for cp in copies:
        cp.wait()
    tail = kv_s[:, :, 512:528, :].astype(F32)
    used = lax.broadcasted_iota(jnp.int32, tail.shape, 2) < 2
    c1 = jnp.sum(jnp.where(used & (tail < 0.5), 1.0, 0.0)).astype(jnp.int32)
    c2 = jnp.sum(jnp.where(used & (tail < 1.5), 1.0, 0.0)).astype(jnp.int32)
    first = y * (8 * TOK) + z * (2 * TOK) + c * TOK
    last = first + TOK - 1
    start = jnp.where(ids[...] == 0, 0, jnp.where(ids[...] == 1, c1, c2))
    lo_start = jnp.where(first >= c2, c2, jnp.where(first >= c1, c1, 0))
    hi_start = jnp.where(last >= c2, c2, jnp.where(last >= c1, c1, 0))
    diag = first // BK
    lo = lo_start // BK
    full = jnp.clip((hi_start + BK - 1) // BK, lo, diag)
    pos = first + lax.broadcasted_iota(jnp.int32, (1, TOK), 1)

    def block(j, masked, causal):
        kb = kv_s[0, j, 0:BK, :]
        vt = jnp.concatenate([kv_s[1, j, 128 * n:128 * n + 128, :] for n in range(4)], axis=1)
        if masked or causal:
            kpos = j * BK + lax.broadcasted_iota(jnp.int32, (BK, TOK), 0)
            ok = kpos >= start
            if causal:
                ok = ok & (kpos <= pos)

        def score(h):
            s = lax.dot_general(kb, q_s[h], (((1,), (1,)), ((), ())), preferred_element_type=F32)
            return jnp.where(ok, s, NEG) if masked or causal else s

        s_next = score(0)
        for h in range(GQA):
            s = s_next
            if h + 1 < GQA:
                s_next = score(h + 1)
            m_old = m_s[h:h + 1, :]
            m_new = jnp.maximum(m_old, jnp.max(s, axis=0, keepdims=True))
            p = jnp.exp2(s - m_new)
            alpha = jnp.exp2(m_old - m_new)
            m_s[h:h + 1, :] = m_new
            l_s[h:h + 1, :] = l_s[h:h + 1, :] * alpha + jnp.sum(p, axis=0, keepdims=True)
            acc_s[h] = acc_s[h] * alpha + jnp.dot(vt, p.astype(BF), preferred_element_type=F32)

    def loop(lo_, hi_, masked):
        def body_(j, carry):
            block(j, masked, False)
            return carry

        lax.fori_loop(lo_, hi_, body_, 0)

    loop(lo, full, True)
    loop(full, diag, False)
    block(diag, True, True)
    for h in range(GQA):
        out[h] = jnp.transpose(acc_s[h] / l_s[h:h + 1, :]).astype(BF)


def attend(info, q_in, q_got, bias, cos, sin, ids, kv):
    vm = pl.BlockSpec(memory_space=pltpu.VMEM)
    hb = pl.BlockSpec(memory_space=pl.ANY)
    return pl.pallas_call(
        attend_kernel,
        out_shape=jax.ShapeDtypeStruct((GQA, TOK, HEAD_DIM), BF),
        in_specs=[pl.BlockSpec(memory_space=pltpu.SMEM)] + [vm] * 6 + [hb] * 8,
        out_specs=vm,
        scratch_shapes=[
            pltpu.VMEM((2, 16, PAY, HEAD_DIM), BF),
            pltpu.VMEM((GQA, TOK, HEAD_DIM), BF),
            pltpu.VMEM((GQA, TOK), F32),
            pltpu.VMEM((GQA, TOK), F32),
            pltpu.VMEM((GQA, HEAD_DIM, TOK), F32),
            pltpu.SemaphoreType.DMA((2,)),
        ],
        cost_estimate=pl.CostEstimate(flops=10 ** 10, bytes_accessed=6 << 20, transcendentals=10 ** 7),
        name="attend",
    )(info, q_in, q_got, bias, cos, sin, ids, *kv)


def kv_kernel(info, mine, got, bias, cos, sin, idrow, out):
    u = mine[...] + got[...]

    @pl.when(info[3] == 0)
    def _():
        out[0:512, :] = rope(u + bias[:, :HEAD_DIM].astype(F32), cos[...], sin[...]).astype(BF)

    @pl.when(info[3] == 1)
    def _():
        v = u + bias[:, HEAD_DIM:].astype(F32)
        for n in range(4):
            out[n * 128:(n + 1) * 128, :] = jnp.transpose(v[n * 128:(n + 1) * 128, :]).astype(BF)

    sel = lax.broadcasted_iota(jnp.int32, (16, HEAD_DIM), 0) == 0
    r0 = jnp.broadcast_to(idrow[0:1, :], (16, HEAD_DIM)).astype(F32)
    r1 = jnp.broadcast_to(idrow[1:2, :], (16, HEAD_DIM)).astype(F32)
    out[512:528, :] = jnp.where(sel, r0, r1).astype(BF)


def mix_kernel(info, *refs, plan, last):
    atts, refs = refs[:len(plan) + last], refs[len(plan) + last:]
    acc, refs = (refs[0], refs[1:]) if last else (None, refs)
    ds = sorted({d for _, use in plan for d in use})
    w, (out, w0, w1, tot, att, sems) = refs[:4 * len(ds)], refs[4 * len(ds):]
    x, y, z, c = (info[i] for i in range(4))
    terms = [(i, k, d) for i, (k, use) in enumerate(plan) for d in use]
    by_d = [[t for t in terms if t[2] == d] for d in ds]
    spot1 = {t: sum(len(g) for g in by_d[:m]) + g.index(t) for m, g in enumerate(by_d) for t in g}
    for side in range(2):
        for is_one in range(2):
            @pl.when((c if side == 0 else 1 - c) == is_one)
            def _(side=side, is_one=is_one):
                for at, t in enumerate(terms):
                    for n in range(4):
                        src = w[(side * len(ds) + ds.index(t[2])) * 2 + n // 2].at[n % 2, lax.rem(x + t[1], 4)]
                        dst = w1.at[pl.ds((spot1[t] * 4 + n) * 128, 128)] if is_one else w0.at[n, pl.ds(at * 128, 128)]
                        pltpu.make_async_copy(src, dst, sems.at[is_one]).start()
    for i, (k, _) in enumerate(plan):
        if k == 2:
            for m in range(2):
                att[i, m * 4:m * 4 + 4] = atts[i + m][...]
        else:
            att[i] = atts[i][...]
    for cc in range(4):
        col = slice(cc * 512, cc * 512 + 512)
        tot[cc] = acc[:, col] if last else jnp.zeros((TOK, 512), F32)
    pltpu.make_async_copy(w0, w0, sems.at[0]).wait()
    lhs = jnp.concatenate([att[i, lax.rem(z + d, 4) * 2] for i, k, d in terms], axis=1)
    for n in range(4):
        tot[lax.rem(y + OFFS[n], 4)] += jnp.dot(lhs, w0[n], preferred_element_type=F32)
    pltpu.make_async_copy(w1, w1, sems.at[1]).wait()
    row = 0
    for d, g in zip(ds, by_d):
        lhs = jnp.concatenate([att[i, lax.rem(z + o, 4) * 2 + 1] for i, k, _ in g for o in OFFS], axis=1)
        tot[lax.rem(y + d, 4)] += jnp.dot(lhs, w1[row:row + 512 * len(g), :], preferred_element_type=F32)
        row += 512 * len(g)
    for cc in range(4):
        out[:, cc * 512:cc * 512 + 512] = tot[cc].astype(out.dtype)


def mix(info, atts, acc, w, plan):
    vm = pl.BlockSpec(memory_space=pltpu.VMEM)
    last = acc is not None
    args = (info, *atts, *((acc,) if last else ()))
    work = sum(len(use) for _, use in plan)
    return pl.pallas_call(
        functools.partial(mix_kernel, plan=plan, last=last),
        out_shape=jax.ShapeDtypeStruct((TOK, 2048), BF if last else F32),
        in_specs=[pl.BlockSpec(memory_space=pltpu.SMEM)] + [vm] * (len(args) - 1) + [pl.BlockSpec(memory_space=pl.ANY)] * len(w),
        out_specs=vm,
        scratch_shapes=[
            pltpu.VMEM((4, work * 128, 512), BF), pltpu.VMEM((work * 512, 512), BF), pltpu.VMEM((4, TOK, 512), F32),
            pltpu.VMEM((len(plan), GQA, TOK, 128), BF), pltpu.SemaphoreType.DMA((2,))],
        cost_estimate=pl.CostEstimate(flops=work * 2 ** 28, bytes_accessed=work << 20, transcendentals=0),
        name="mix",
    )(*args, *w)


def layer(tokens, proj_weight, proj_bias, out_weight, doc_ids):
    x, y, z, c = (lax.axis_index(n) for n in ("grp", "y", "z", "c"))
    quarter = lax.dynamic_slice(tokens.reshape(16, 4, 128, 256), (0, x, 0, 0), (16, 1, 128, 256)).reshape(16, 128, 256)
    got = lax.all_to_all(quarter, ("y", "z"), split_axis=0, concat_axis=0, tiled=True)
    near_w, far_w = plane_gather(proj_weight)
    rows = lax.dynamic_slice_in_dim(out_weight, (2 * z + c) * 128, 128, axis=0)
    share = jnp.stack([lax.dynamic_slice_in_dim(rows, n * 2048 + y * 512, 512, axis=1) for n in range(4)])
    share = lax.all_to_all(share, "grp", split_axis=0, concat_axis=0, tiled=True)
    near_o, far_o = plane_gather(share)
    got = got.reshape(4, 4, 128, 256)
    got = lax.dynamic_slice_in_dim(jnp.concatenate([got, got], axis=0), y, 4, axis=0)
    got = lax.dynamic_slice_in_dim(jnp.concatenate([got, got], axis=1), z, 4, axis=1)
    got = jnp.where(c == 0, got, jnp.transpose(got, (1, 0, 2, 3)))
    g = jnp.stack([got[0], got[3]]), jnp.stack([got[1], got[2]])
    t_m, t_p = [hop(v, "grp", 1) for v in g], [hop(v, "grp", -1) for v in g]
    t_f = hop(t_m[0], "grp", 1), hop(t_p[1], "grp", -1)
    ts = (*g, *t_p, *t_f, *t_m)
    info = jnp.stack([x, y, z, c]).astype(jnp.int32)
    acc = near_project(ts, near_w)
    kv_mine, kv_other = far_project(info, ts, far_w, acc, True)
    kv_got = swap(kv_other)
    q_mine, q_other = far_project(info, ts, far_w, acc, False)
    q_got = swap(q_other)
    bias = proj_bias.reshape(1, COLS)
    inverse_freq = theta_base ** (-(jnp.arange(HEAD_DIM // 2, dtype=F32) * 2.0) / HEAD_DIM)
    chip = y * (8 * TOK) + z * (2 * TOK)
    angles = (chip + jnp.arange(2 * TOK, dtype=jnp.int32)).astype(F32)[:, None] * inverse_freq[None, :]
    cos = jnp.concatenate([jnp.cos(angles), jnp.cos(angles)], axis=1)
    sin = jnp.concatenate([jnp.sin(angles), jnp.sin(angles)], axis=1)
    cos_q, sin_q = (lax.dynamic_slice_in_dim(t, c * TOK, TOK, axis=0) for t in (cos, sin))
    vm = pl.BlockSpec(memory_space=pltpu.VMEM)
    payload = pl.pallas_call(
        kv_kernel, out_shape=jax.ShapeDtypeStruct((PAY, HEAD_DIM), BF), name="kv",
        in_specs=[pl.BlockSpec(memory_space=pltpu.SMEM)] + [vm] * 6, out_specs=vm)(
        info, kv_mine, kv_got, bias[:, 1024:], cos, sin, doc_ids.reshape(2, 128))
    line = line_gather(payload)
    km, kp, kf = turn(line, 1, True), turn(line, -1, True), turn(line, 2, True)
    mine = (line, km, kp, kf)
    other = (swap(line),)
    other += tuple(swap(p) for p in mine[1:])
    attended = attend(info, q_mine, q_got, bias[:, :1024], cos_q, sin_q, doc_ids.reshape(1, TOK), mine + other)
    w_near = near_o[:2] + near_o[4:] + near_o[2:4]
    near_w2 = w_near + tuple(swap(p) for p in w_near)
    far_pair = far_o + tuple(swap(p) for p in far_o)
    a_m, a_p = hop(attended, "grp", 1), hop(attended, "grp", -1)
    a_f = hop(a_m[:4], "grp", 1), hop(a_p[4:], "grp", -1)
    atts = (attended, a_p, a_m)
    acc = mix(info, atts, None, near_w2, ((0, (0, 1, 3)), (1, (0, 1, 3)), (3, (0, 1, 3))))
    w_all = near_w2[:4] + far_pair[:2] + near_w2[4:6] + near_w2[6:10] + far_pair[2:] + near_w2[10:]
    return mix(info, atts + a_f, acc, w_all, ((0, (2,)), (1, (2,)), (3, (2,)), (2, (0, 1, 2, 3))))


def solution(mesh):
    fine = Mesh(mesh.devices.reshape(4, 4, 4, 2), ("grp", "y", "z", "c"))
    seq = ("y", "z", "c")
    return jax.shard_map(
        layer,
        mesh=fine,
        in_specs=(P(None, seq), P(seq, "grp"), P("grp"), P("grp", None), P(seq)),
        out_specs=P(seq, "grp"),
        check_vma=False,
    )
```

time: 275 us -> 252 us (0.916)
  the two profiles are of different devices: /device:TPU:24 before, /device:TPU:17 now
where the time goes in v2:
time: 252 us
  starting transfers between devices  96.3 us (38%)
  waiting for transfers between devices  85.2 us (34%)
  Pallas kernels  48.1 us (19%)
  other arithmetic  12.1 us (5%)
  local copies, waits for them, and re-layouts  9.56 us (4%)
    ppermute x24, starting transfers between devices, hop(): return lax.ppermute(x, axis, [(i, (i + k) % n) for i in range(n)])  57.2 us
    ppermute x24, waiting for transfers between devices, turn(): return lax.ppermute(x, ('y', 'z', 'c'), pairs)  51.2 us
    ppermute x24, starting transfers between devices, turn(): return lax.ppermute(x, ('y', 'z', 'c'), pairs)  29.4 us
    ppermute x24, waiting for transfers between devices, hop(): return lax.ppermute(x, axis, [(i, (i + k) % n) for i in range(n)])  21.1 us
    pallas_call x2, Pallas kernels, mix(): pl.pallas_call(functools.partial(mix_kernel, plan=plan, last=last), out_s...  18.5 us
    pallas_call x1, Pallas kernels, near_project(): pl.pallas_call(near_kernel, out_shape=jax.ShapeDtypeStruct((512, COLS), F...  10 us
    pallas_call x2, Pallas kernels, far_project(): pl.pallas_call(functools.partial(far_kernel, kv=kv), out_shape=(half, hal...  9.87 us
    pallas_call x1, Pallas kernels, attend(): pl.pallas_call(attend_kernel, out_shape=jax.ShapeDtypeStruct((GQA, TOK, H...  7.75 us
  transfers between devices with their start and end apart: 50, of which 12 were waited for; matrix products, arithmetic and copies ran while one was open for 7% of the time, Pallas kernels for 16%

profile of v2, /device:TPU:17, one launch (start us, length us, event | category | flops | bytes accessed | tf_op | source)
XLA Modules:
  0.0 251.8 jit_solution(1551760310735815689)
XLA Ops:
  8.1 4.0 %all-to-all-start.1 = ((bf16[4,128,512]{2,1,0:T(8,128)(2,1)}), bf16[4,128,512]{2,1,0:T(8,128)(2,1)S(1)}, u32[]{:S(2)}, u32[]{:S(2)}) async-start(bf16[4,128,512]{2,1,0:T(8,128)(2,1)} %pad_maximum_fusion.6), calls=%async_computation.1 | async-start | bytes 1048576 | tf_op jit(solution)/shard_map/all_to_all | solution.py:325
  14.6 6.0 %all-to-all-done.1 = bf16[4,128,512]{2,1,0:T(8,128)(2,1)S(1)} async-done(((bf16[4,128,512]{2,1,0:T(8,128)(2,1)}), bf16[4,128,512]{2,1,0:T(8,128)(2,1)S(1)}, u32[]{:S(2)}, u32[]{:S(2)}) %all-to-all-start.1) | async-done | bytes 524320 | tf_op jit(solution)/shard_map/all_to_all | solution.py:325
  20.5 5.6 %all-to-all-start = ((bf16[16,128,256]{2,1,0:T(8,128)(2,1)}), bf16[16,128,256]{2,1,0:T(8,128)(2,1)S(1)}, u32[]{:S(2)}, u32[]{:S(2)}) async-start(bf16[16,128,256]{2,1,0:T(8,128)(2,1)} %dynamic-slice_bitcast_fusion), calls=%async_computation | async-start | bytes 2097152 | tf_op jit(solution)/shard_map/all_to_all | solution.py:321
  32.8 6.9 %all-to-all-done = bf16[16,128,256]{2,1,0:T(8,128)(2,1)S(1)} async-done(((bf16[16,128,256]{2,1,0:T(8,128)(2,1)}), bf16[16,128,256]{2,1,0:T(8,128)(2,1)S(1)}, u32[]{:S(2)}, u32[]{:S(2)}) %all-to-all-start) | async-done | bytes 1048608 | tf_op jit(solution)/shard_map/all_to_all | solution.py:321
  41.5 10.7 %collective-permute-done.31 = bf16[4,128,512]{2,1,0:T(8,128)(2,1)S(1)} collective-permute-done((bf16[4,128,512]{2,1,0:T(8,128)(2,1)S(1)}, bf16[4,128,512]{2,1,0:T(8,128)(2,1)S(1)}, u32[]{:S(2)}, u32[]{:S(2)}) %collective-permute-start.31) | collective-permute-done | bytes 524320 | tf_op jit(solution)/shard_map/ppermute | solution.py:40
  53.7 7.2 %collective-permute-done.9.refs_10_ = bf16[2,256,1280]{2,1,0:T(8,128)(2,1)} collective-permute-done((bf16[2,256,1280]{2,1,0:T(8,128)(2,1)S(1)}, bf16[2,256,1280]{2,1,0:T(8,128)(2,1)}, u32[]{:S(2)}, u32[]{:S(2)}) %collective-permute-start.9) | collective-permute-done | bytes 1310752 | tf_op jit(solution)/shard_map/ppermute | solution.py:40
  63.9 14.6 %collective-permute-done.10.refs_11_ = bf16[2,256,1280]{2,1,0:T(8,128)(2,1)} collective-permute-done((bf16[2,256,1280]{2,1,0:T(8,128)(2,1)}, bf16[2,256,1280]{2,1,0:T(8,128)(2,1)}, u32[]{:S(2)}, u32[]{:S(2)}) %collective-permute-start.10) | collective-permute-done | bytes 1310752 | tf_op jit(solution)/shard_map/ppermute | solution.py:40
  83.9 5.7 %collective-permute-done.refs_2_ = bf16[2,4,128,256]{3,2,1,0:T(8,128)(2,1)S(1)} collective-permute-done((bf16[2,4,128,256]{3,2,1,0:T(8,128)(2,1)S(1)}, bf16[2,4,128,256]{3,2,1,0:T(8,128)(2,1)S(1)}, u32[]{:S(2)}, u32[]{:S(2)}) %collective-permute-start) | collective-permute-done | bytes 524320 | tf_op jit(solution)/shard_map/ppermute | solution.py:25
  91.7 9.1 %collective-permute-done.1.refs_3_ = bf16[2,4,128,256]{3,2,1,0:T(8,128)(2,1)} collective-permute-done((bf16[2,4,128,256]{3,2,1,0:T(8,128)(2,1)}, bf16[2,4,128,256]{3,2,1,0:T(8,128)(2,1)}, u32[]{:S(2)}, u32[]{:S(2)}) %collective-permute-start.1) | collective-permute-done | bytes 524320 | tf_op jit(solution)/shard_map/ppermute | solution.py:25
  107.4 4.5 %collective-permute-done.3.refs_4_ = bf16[2,4,128,256]{3,2,1,0:T(8,128)(2,1)} collective-permute-done((bf16[2,4,128,256]{3,2,1,0:T(8,128)(2,1)}, bf16[2,4,128,256]{3,2,1,0:T(8,128)(2,1)}, u32[]{:S(2)}, u32[]{:S(2)}) %collective-permute-start.3) | collective-permute-done | bytes 524320 | tf_op jit(solution)/shard_map/ppermute | solution.py:25
  113.4 10.0 %near.1.refs_10_ = f32[512,1280]{1,0:T(8,128)} custom-call(bf16[2,4,128,256]{3,2,1,0:T(8,128)(2,1)} %copy-done.3, bf16[2,4,128,256]{3,2,1,0:T(8,128)(2,1)} %stack.116.refs_1_, bf16[2,4,128,256]{3,2,1,0:T(8,128)(2,1)} %copy-done.10, bf16[2,4,128,256]{3,2,1,0:T(8,128)(2,1)} %collective-permute-done.1.refs_3_, ...), custom_call_target="tpu_custom_call" | custom-call | flops 4026531840 | bytes 14680064 | tf_op jit(solution)/shard_map/near/pallas_call | solution.py:79
  124.5 3.6 %far_kv.1 = (f32[512,128]{1,0:T(8,128)}, f32[512,128]{1,0:T(8,128)}) custom-call(s32[4]{0:T(128)} %pad_add_fusion.info, bf16[2,4,128,256]{3,2,1,0:T(8,128)(2,1)} %copy-done.3, bf16[2,4,128,256]{3,2,1,0:T(8,128)(2,1)} %stack.116.refs_1_, bf16[2,4,128,256]{3,2,1,0:T(8,128)(2,1)} %copy-done.10, bf16[2,4,128,256]{3,2,1,0:T(8,128)(2,1)} %collective-permute-done.1.refs_3_, ...), custom_call_target="tpu_custom_call" | custom-call | flops 268435456 | bytes 5242880 | tf_op jit(solution)/shard_map/far_kv/pallas_call | solution.py:122
  128.1 7.8 %collective-permute-start.16 = (f32[512,128]{1,0:T(8,128)}, f32[512,128]{1,0:T(8,128)}, u32[]{:S(2)}, u32[]{:S(2)}) collective-permute-start(f32[512,128]{1,0:T(8,128)} %get-tuple-element.30), channel_id=1, source_target_pairs={{0,1},{1,0},{2,3},{3,2},{4,5},{5,4},{6,7},{7,6},{8,9},{9,8},{10,11... | collective-permute-start | bytes 786440 | tf_op jit(solution)/shard_map/ppermute | solution.py:25
  142.5 3.8 %collective-permute-done.19 = bf16[528,128]{1,0:T(8,128)(2,1)} collective-permute-done((bf16[528,128]{1,0:T(8,128)(2,1)}, bf16[528,128]{1,0:T(8,128)(2,1)}, u32[]{:S(2)}, u32[]{:S(2)}) %collective-permute-start.19) | collective-permute-done | bytes 135200 | tf_op jit(solution)/shard_map/ppermute | solution.py:40
  146.3 4.4 %collective-permute-start.18 = (bf16[528,128]{1,0:T(8,128)(2,1)}, bf16[528,128]{1,0:T(8,128)(2,1)}, u32[]{:S(2)}, u32[]{:S(2)}) collective-permute-start(bf16[528,128]{1,0:T(8,128)(2,1)} %kv.1), channel_id=1, source_target_pairs={{0,24},{1,7},{2,26},{3,1},{4,28},{5,3},{6,30},{7,5},{8,0},{9,15},{... | collective-permute-start | bytes 405512 | tf_op jit(solution)/shard_map/ppermute | solution.py:40
  150.7 3.7 %collective-permute-done.18 = bf16[528,128]{1,0:T(8,128)(2,1)} collective-permute-done((bf16[528,128]{1,0:T(8,128)(2,1)}, bf16[528,128]{1,0:T(8,128)(2,1)}, u32[]{:S(2)}, u32[]{:S(2)}) %collective-permute-start.18) | collective-permute-done | bytes 135200 | tf_op jit(solution)/shard_map/ppermute | solution.py:40
  154.6 6.3 %far_q.1 = (f32[256,1024]{1,0:T(8,128)}, f32[256,1024]{1,0:T(8,128)}) custom-call(s32[4]{0:T(128)} %pad_add_fusion.info, bf16[2,4,128,256]{3,2,1,0:T(8,128)(2,1)} %copy-done.3, bf16[2,4,128,256]{3,2,1,0:T(8,128)(2,1)} %stack.116.refs_1_, bf16[2,4,128,256]{3,2,1,0:T(8,128)(2,1)} %copy-done.10, bf16[2,4,128,256]{3,2,1,0:T(8,128)(2,1)} %collective-permute-done.1.refs_3_, ...), custom_call_target="tpu_custom_call" | custom-call | flops 1073741824 | bytes 5242880 | tf_op jit(solution)/shard_map/far_q/pallas_call | solution.py:122
  160.8 5.4 %collective-permute-start.15 = (f32[256,1024]{1,0:T(8,128)}, f32[256,1024]{1,0:T(8,128)}, u32[]{:S(2)}, u32[]{:S(2)}) collective-permute-start(f32[256,1024]{1,0:T(8,128)} %get-tuple-element.28), channel_id=1, source_target_pairs={{0,1},{1,0},{2,3},{3,2},{4,5},{5,4},{6,7},{7,6},{8,9},{9,8},{10,11... | collective-permute-start | bytes 3145736 | tf_op jit(solution)/shard_map/ppermute | solution.py:25
  171.5 11.2 %collective-permute-done.20.refs_1_ = bf16[4,528,128]{2,1,0:T(8,128)(2,1)} collective-permute-done((bf16[4,528,128]{2,1,0:T(8,128)(2,1)}, bf16[4,528,128]{2,1,0:T(8,128)(2,1)}, u32[]{:S(2)}, u32[]{:S(2)}) %collective-permute-start.20) | collective-permute-done | bytes 540704 | tf_op jit(solution)/shard_map/ppermute | solution.py:40
  190.0 7.7 %attend.1.refs_0_ = bf16[8,256,128]{2,1,0:T(8,128)(2,1)} custom-call(s32[4]{0:T(128)} %pad_add_fusion.info, f32[256,1024]{1,0:T(8,128)} %get-tuple-element.27.q_in, f32[256,1024]{1,0:T(8,128)} %collective-permute-done.15.q_got, bf16[1,1024]{1,0:T(2,128)(2,1)} %slice.29.bias, f32[256,128]{1,0:T(8,128)} %get-tuple-element.46.cos, ...), custom_call_target="tpu_custom_call" | custom-call | flops 10000000000 | bytes 6291456 | tf_op jit(solution)/shard_map/attend/pallas_call | solution.py:222
  199.3 18.6 %collective-permute-start.41 = (bf16[2,4,128,512]{3,2,1,0:T(8,128)(2,1)S(1)}, bf16[2,4,128,512]{3,2,1,0:T(8,128)(2,1)S(1)}, u32[]{:S(2)}, u32[]{:S(2)}) collective-permute-start(bf16[2,4,128,512]{3,2,1,0:T(8,128)(2,1)S(1)} %collective-permute-done.37.refs_6_.refs_9_), channel_id=1, source_target_pairs={{0,1},{1,0},{2,3},{3,2},{4,5},{5,4},{6,7},{7,6},{8,9},{9,8},{10,11... | collective-permute-start | bytes 3145736 | tf_op jit(solution)/shard_map/ppermute | solution.py:25
  218.4 6.8 %collective-permute-start.46 = (bf16[2,4,128,512]{3,2,1,0:T(8,128)(2,1)}, bf16[2,4,128,512]{3,2,1,0:T(8,128)(2,1)}, u32[]{:S(2)}, u32[]{:S(2)}) collective-permute-start(bf16[2,4,128,512]{3,2,1,0:T(8,128)(2,1)} %collective-permute-done.44.refs_10_), channel_id=1, source_target_pairs={{0,1},{1,0},{2,3},{3,2},{4,5},{5,4},{6,7},{7,6},{8,9},{9,8},{10,11... | collective-permute-start | bytes 3145736 | tf_op jit(solution)/shard_map/ppermute | solution.py:25
  231.6 9.5 %mix.2.refs_5_ = f32[256,2048]{1,0:T(8,128)} custom-call(s32[4]{0:T(128)} %pad_add_fusion.info, bf16[8,256,128]{2,1,0:T(8,128)(2,1)} %attend.1.refs_0_, bf16[8,256,128]{2,1,0:T(8,128)(2,1)} %copy-done.7, bf16[8,256,128]{2,1,0:T(8,128)(2,1)} %copy-done.8, bf16[2,4,128,512]{3,2,1,0:T(8,128)(2,1)} %copy-done, bf16[2,4,128,512]{3,2,1,0:T(8,128)(2,1)} %copy-done.1, ...), custom_call_target="tpu_custom_call" | custom-call | flops 2415919104 | bytes 9437184 | tf_op jit(solution)/shard_map/mix/pallas_call | solution.py:305
  242.6 9.0 %mix.3 = bf16[256,2048]{1,0:T(8,128)(2,1)} custom-call(s32[4]{0:T(128)} %pad_add_fusion.info, bf16[8,256,128]{2,1,0:T(8,128)(2,1)} %attend.1.refs_0_, bf16[8,256,128]{2,1,0:T(8,128)(2,1)} %copy-done.7, bf16[8,256,128]{2,1,0:T(8,128)(2,1)} %copy-done.8, bf16[4,256,128]{2,1,0:T(8,128)(2,1)} %copy-done.19, bf16[4,256,128]{2,1,0:T(8,128)(2,1)} %copy-done.20, ...), custom_call_target="tpu_custom_call" | custom-call | flops 1879048192 | bytes 7340032 | tf_op jit(solution)/shard_map/mix/pallas_call | solution.py:305
  (152 shorter events, 69.1 us)
Async XLA Ops:
  1.6 24.5 %collective-permute-start.8 = (bf16[256,1280]{1,0:T(8,128)(2,1)}, bf16[256,1280]{1,0:T(8,128)(2,1)}, u32[]{:S(2)}, u32[]{:S(2)}) collective-permute-start(bf16[256,1280]{1,0:T(8,128)(2,1)} %param.6), channel_id=1, source_target_pairs={{0,16},{1,5},{2,18},{3,7},{4,20},{5,1},{6,22},{7,3},{8,24},{9,13},... | collective-permute-start | bytes 1966088 | tf_op jit(solution)/shard_map/ppermute | solution.py:40
  4.9 21.2 %collective-permute-start.7 = (bf16[256,1280]{1,0:T(8,128)(2,1)}, bf16[256,1280]{1,0:T(8,128)(2,1)}, u32[]{:S(2)}, u32[]{:S(2)}) collective-permute-start(bf16[256,1280]{1,0:T(8,128)(2,1)} %param.6), channel_id=1, source_target_pairs={{0,24},{1,7},{2,26},{3,1},{4,28},{5,3},{6,30},{7,5},{8,0},{9,15},{... | collective-permute-start | bytes 1966088 | tf_op jit(solution)/shard_map/ppermute | solution.py:40
  28.7 32.1 %collective-permute-start.9 = (bf16[2,256,1280]{2,1,0:T(8,128)(2,1)S(1)}, bf16[2,256,1280]{2,1,0:T(8,128)(2,1)}, u32[]{:S(2)}, u32[]{:S(2)}) collective-permute-start(bf16[2,256,1280]{2,1,0:T(8,128)(2,1)S(1)} %pad_maximum_fusion.refs_8_), channel_id=1, source_target_pairs={{0,2},{1,9},{2,4},{3,11},{4,6},{5,13},{6,0},{7,15},{8,10},{9,17},{... | collective-permute-start | bytes 3932168 | tf_op jit(solution)/shard_map/ppermute | solution.py:40
  29.6 48.9 %collective-permute-start.10 = (bf16[2,256,1280]{2,1,0:T(8,128)(2,1)}, bf16[2,256,1280]{2,1,0:T(8,128)(2,1)}, u32[]{:S(2)}, u32[]{:S(2)}) collective-permute-start(bf16[2,256,1280]{2,1,0:T(8,128)(2,1)} %pad_maximum_fusion.1.refs_9_), channel_id=1, source_target_pairs={{0,2},{1,9},{2,4},{3,11},{4,6},{5,13},{6,0},{7,15},{8,10},{9,17},{... | collective-permute-start | bytes 3932168 | tf_op jit(solution)/shard_map/ppermute | solution.py:40
  29.7 50.0 %collective-permute-start.11 = (bf16[2,256,1280]{2,1,0:T(8,128)(2,1)S(1)}, bf16[2,256,1280]{2,1,0:T(8,128)(2,1)}, u32[]{:S(2)}, u32[]{:S(2)}) collective-permute-start(bf16[2,256,1280]{2,1,0:T(8,128)(2,1)S(1)} %pad_maximum_fusion.refs_8_), channel_id=1, source_target_pairs={{0,6},{1,25},{2,0},{3,27},{4,2},{5,29},{6,4},{7,31},{8,14},{9,1},{... | collective-permute-start | bytes 3932168 | tf_op jit(solution)/shard_map/ppermute | solution.py:40
  31.1 48.9 %collective-permute-start.12 = (bf16[2,256,1280]{2,1,0:T(8,128)(2,1)}, bf16[2,256,1280]{2,1,0:T(8,128)(2,1)}, u32[]{:S(2)}, u32[]{:S(2)}) collective-permute-start(bf16[2,256,1280]{2,1,0:T(8,128)(2,1)} %pad_maximum_fusion.1.refs_9_), channel_id=1, source_target_pairs={{0,6},{1,25},{2,0},{3,27},{4,2},{5,29},{6,4},{7,31},{8,14},{9,1},{... | collective-permute-start | bytes 3932168 | tf_op jit(solution)/shard_map/ppermute | solution.py:40
  31.7 20.5 %collective-permute-start.31 = (bf16[4,128,512]{2,1,0:T(8,128)(2,1)S(1)}, bf16[4,128,512]{2,1,0:T(8,128)(2,1)S(1)}, u32[]{:S(2)}, u32[]{:S(2)}) collective-permute-start(bf16[4,128,512]{2,1,0:T(8,128)(2,1)S(1)} %all-to-all-done.1), channel_id=1, source_target_pairs={{0,8},{1,3},{2,10},{3,5},{4,12},{5,7},{6,14},{7,1},{8,16},{9,11},{... | collective-permute-start | bytes 1572872 | tf_op jit(solution)/shard_map/ppermute | solution.py:40
  52.2 30.2 %collective-permute-start.33 = (bf16[4,128,512]{2,1,0:T(8,128)(2,1)S(1)}, bf16[4,128,512]{2,1,0:T(8,128)(2,1)S(1)}, u32[]{:S(2)}, u32[]{:S(2)}) collective-permute-start(bf16[4,128,512]{2,1,0:T(8,128)(2,1)S(1)} %all-to-all-done.1), channel_id=1, source_target_pairs={{0,16},{1,5},{2,18},{3,7},{4,20},{5,1},{6,22},{7,3},{8,24},{9,13},... | collective-permute-start | bytes 1572872 | tf_op jit(solution)/shard_map/ppermute | solution.py:40
  60.8 22.9 %collective-permute-start.32 = (bf16[4,128,512]{2,1,0:T(8,128)(2,1)S(1)}, bf16[4,128,512]{2,1,0:T(8,128)(2,1)S(1)}, u32[]{:S(2)}, u32[]{:S(2)}) collective-permute-start(bf16[4,128,512]{2,1,0:T(8,128)(2,1)S(1)} %all-to-all-done.1), channel_id=1, source_target_pairs={{0,24},{1,7},{2,26},{3,1},{4,28},{5,3},{6,30},{7,5},{8,0},{9,15},{... | collective-permute-start | bytes 1572872 | tf_op jit(solution)/shard_map/ppermute | solution.py:40
  80.0 20.8 %collective-permute-start.1 = (bf16[2,4,128,256]{3,2,1,0:T(8,128)(2,1)}, bf16[2,4,128,256]{3,2,1,0:T(8,128)(2,1)}, u32[]{:S(2)}, u32[]{:S(2)}) collective-permute-start(bf16[2,4,128,256]{3,2,1,0:T(8,128)(2,1)} %stack.116.refs_1_), channel_id=1, source_target_pairs={{0,96},{32,0},{64,32},{96,64},{1,97},{33,1},{65,33},{97,65},{2,98}... | collective-permute-start | bytes 1572872 | tf_op jit(solution)/shard_map/ppermute | solution.py:25
  82.4 41.0 %collective-permute-start.13 = (bf16[2,256,1280]{2,1,0:T(8,128)(2,1)}, bf16[2,256,1280]{2,1,0:T(8,128)(2,1)S(1)}, u32[]{:S(2)}, u32[]{:S(2)}) collective-permute-start(bf16[2,256,1280]{2,1,0:T(8,128)(2,1)} %collective-permute-done.9.refs_10_), channel_id=1, source_target_pairs={{0,2},{1,9},{2,4},{3,11},{4,6},{5,13},{6,0},{7,15},{8,10},{9,17},{... | collective-permute-start | bytes 3932168 | tf_op jit(solution)/shard_map/ppermute | solution.py:40
  83.7 39.7 %collective-permute-start.14 = (bf16[2,256,1280]{2,1,0:T(8,128)(2,1)}, bf16[2,256,1280]{2,1,0:T(8,128)(2,1)}, u32[]{:S(2)}, u32[]{:S(2)}) collective-permute-start(bf16[2,256,1280]{2,1,0:T(8,128)(2,1)} %collective-permute-done.12.refs_13_), channel_id=1, source_target_pairs={{0,6},{1,25},{2,0},{3,27},{4,2},{5,29},{6,4},{7,31},{8,14},{9,1},{... | collective-permute-start | bytes 3932168 | tf_op jit(solution)/shard_map/ppermute | solution.py:40
  91.7 20.1 %collective-permute-start.3 = (bf16[2,4,128,256]{3,2,1,0:T(8,128)(2,1)}, bf16[2,4,128,256]{3,2,1,0:T(8,128)(2,1)}, u32[]{:S(2)}, u32[]{:S(2)}) collective-permute-start(bf16[2,4,128,256]{3,2,1,0:T(8,128)(2,1)} %collective-permute-done.2.refs_6_), channel_id=1, source_target_pairs={{0,32},{32,64},{64,96},{96,0},{1,33},{33,65},{65,97},{97,1},{2,34}... | collective-permute-start | bytes 1572872 | tf_op jit(solution)/shard_map/ppermute | solution.py:25
  105.7 62.5 %collective-permute-start.34 = (bf16[2,4,128,512]{3,2,1,0:T(8,128)(2,1)S(1)}, bf16[2,4,128,512]{3,2,1,0:T(8,128)(2,1)}, u32[]{:S(2)}, u32[]{:S(2)}) collective-permute-start(bf16[2,4,128,512]{3,2,1,0:T(8,128)(2,1)S(1)} %pad_maximum_fusion.2.refs_3_.refs_6_), channel_id=1, source_target_pairs={{0,2},{1,9},{2,4},{3,11},{4,6},{5,13},{6,0},{7,15},{8,10},{9,17},{... | collective-permute-start | bytes 3145736 | tf_op jit(solution)/shard_map/ppermute | solution.py:40
  111.8 57.9 %collective-permute-start.36 = (bf16[2,4,128,512]{3,2,1,0:T(8,128)(2,1)S(1)}, bf16[2,4,128,512]{3,2,1,0:T(8,128)(2,1)}, u32[]{:S(2)}, u32[]{:S(2)}) collective-permute-start(bf16[2,4,128,512]{3,2,1,0:T(8,128)(2,1)S(1)} %pad_maximum_fusion.2.refs_3_.refs_6_), channel_id=1, source_target_pairs={{0,6},{1,25},{2,0},{3,27},{4,2},{5,29},{6,4},{7,31},{8,14},{9,1},{... | collective-permute-start | bytes 3145736 | tf_op jit(solution)/shard_map/ppermute | solution.py:40
  112.1 56.4 %collective-permute-start.35 = (bf16[2,4,128,512]{3,2,1,0:T(8,128)(2,1)S(1)}, bf16[2,4,128,512]{3,2,1,0:T(8,128)(2,1)}, u32[]{:S(2)}, u32[]{:S(2)}) collective-permute-start(bf16[2,4,128,512]{3,2,1,0:T(8,128)(2,1)S(1)} %pad_maximum_fusion.3.refs_4_.refs_7_), channel_id=1, source_target_pairs={{0,2},{1,9},{2,4},{3,11},{4,6},{5,13},{6,0},{7,15},{8,10},{9,17},{... | collective-permute-start | bytes 3145736 | tf_op jit(solution)/shard_map/ppermute | solution.py:40
  136.9 33.4 %collective-permute-start.37 = (bf16[2,4,128,512]{3,2,1,0:T(8,128)(2,1)S(1)}, bf16[2,4,128,512]{3,2,1,0:T(8,128)(2,1)S(1)}, u32[]{:S(2)}, u32[]{:S(2)}) collective-permute-start(bf16[2,4,128,512]{3,2,1,0:T(8,128)(2,1)S(1)} %pad_maximum_fusion.3.refs_4_.refs_7_), channel_id=1, source_target_pairs={{0,6},{1,25},{2,0},{3,27},{4,2},{5,29},{6,4},{7,31},{8,14},{9,1},{... | collective-permute-start | bytes 3145736 | tf_op jit(solution)/shard_map/ppermute | solution.py:40
  160.8 25.2 %collective-permute-start.15 = (f32[256,1024]{1,0:T(8,128)}, f32[256,1024]{1,0:T(8,128)}, u32[]{:S(2)}, u32[]{:S(2)}) collective-permute-start(f32[256,1024]{1,0:T(8,128)} %get-tuple-element.28), channel_id=1, source_target_pairs={{0,1},{1,0},{2,3},{3,2},{4,5},{5,4},{6,7},{7,6},{8,9},{9,8},{10,11... | collective-permute-start | bytes 3145736 | tf_op jit(solution)/shard_map/ppermute | solution.py:25
  188.5 29.4 %collective-permute-start.44 = (bf16[2,4,128,512]{3,2,1,0:T(8,128)(2,1)}, bf16[2,4,128,512]{3,2,1,0:T(8,128)(2,1)}, u32[]{:S(2)}, u32[]{:S(2)}) collective-permute-start(bf16[2,4,128,512]{3,2,1,0:T(8,128)(2,1)} %collective-permute-done.34.refs_7_.refs_12_), channel_id=1, source_target_pairs={{0,2},{1,9},{2,4},{3,11},{4,6},{5,13},{6,0},{7,15},{8,10},{9,17},{... | collective-permute-start | bytes 3145736 | tf_op jit(solution)/shard_map/ppermute | solution.py:40
  188.5 29.4 %collective-permute-start.45 = (bf16[2,4,128,512]{3,2,1,0:T(8,128)(2,1)S(1)}, bf16[2,4,128,512]{3,2,1,0:T(8,128)(2,1)}, u32[]{:S(2)}, u32[]{:S(2)}) collective-permute-start(bf16[2,4,128,512]{3,2,1,0:T(8,128)(2,1)S(1)} %collective-permute-done.37.refs_6_.refs_9_), channel_id=1, source_target_pairs={{0,6},{1,25},{2,0},{3,27},{4,2},{5,29},{6,4},{7,31},{8,14},{9,1},{... | collective-permute-start | bytes 3145736 | tf_op jit(solution)/shard_map/ppermute | solution.py:40
  197.7 20.6 %collective-permute-start.27 = (bf16[8,256,128]{2,1,0:T(8,128)(2,1)}, bf16[8,256,128]{2,1,0:T(8,128)(2,1)S(1)}, u32[]{:S(2)}, u32[]{:S(2)}) collective-permute-start(bf16[8,256,128]{2,1,0:T(8,128)(2,1)} %attend.1.refs_0_), channel_id=1, source_target_pairs={{0,96},{32,0},{64,32},{96,64},{1,97},{33,1},{65,33},{97,65},{2,98}... | collective-permute-start | bytes 1572872 | tf_op jit(solution)/shard_map/ppermute | solution.py:25
  199.1 26.1 %collective-permute-start.28 = (bf16[8,256,128]{2,1,0:T(8,128)(2,1)}, bf16[8,256,128]{2,1,0:T(8,128)(2,1)S(1)}, u32[]{:S(2)}, u32[]{:S(2)}) collective-permute-start(bf16[8,256,128]{2,1,0:T(8,128)(2,1)} %attend.1.refs_0_), channel_id=1, source_target_pairs={{0,32},{32,64},{64,96},{96,0},{1,33},{33,65},{65,97},{97,1},{2,34}... | collective-permute-start | bytes 1572872 | tf_op jit(solution)/shard_map/ppermute | solution.py:25
  199.3 29.5 %collective-permute-start.41 = (bf16[2,4,128,512]{3,2,1,0:T(8,128)(2,1)S(1)}, bf16[2,4,128,512]{3,2,1,0:T(8,128)(2,1)S(1)}, u32[]{:S(2)}, u32[]{:S(2)}) collective-permute-start(bf16[2,4,128,512]{3,2,1,0:T(8,128)(2,1)S(1)} %collective-permute-done.37.refs_6_.refs_9_), channel_id=1, source_target_pairs={{0,1},{1,0},{2,3},{3,2},{4,5},{5,4},{6,7},{7,6},{8,9},{9,8},{10,11... | collective-permute-start | bytes 3145736 | tf_op jit(solution)/shard_map/ppermute | solution.py:25
  218.4 22.8 %collective-permute-start.46 = (bf16[2,4,128,512]{3,2,1,0:T(8,128)(2,1)}, bf16[2,4,128,512]{3,2,1,0:T(8,128)(2,1)}, u32[]{:S(2)}, u32[]{:S(2)}) collective-permute-start(bf16[2,4,128,512]{3,2,1,0:T(8,128)(2,1)} %collective-permute-done.44.refs_10_), channel_id=1, source_target_pairs={{0,1},{1,0},{2,3},{3,2},{4,5},{5,4},{6,7},{7,6},{8,9},{9,8},{10,11... | collective-permute-start | bytes 3145736 | tf_op jit(solution)/shard_map/ppermute | solution.py:25
  (48 other events, 704.0 us)
